TPU v7x, 32 devices: a 4x2x2 block of a 4x4x8 slice. The times are simulated.
32 devices in a mesh: dp: 4 (over y, z), tp: 8 (over x, core).
Axes of the slice: x: 4, y: 2, z: 2, core: 2. Of those that a mesh axis runs over, the one named last changes fastest.
The devices are a block of a 4x4x8 slice.
Arguments:
- mel_in: bfloat16 [8, 4096, 80], P('dp', 'tp'), parts along dimension 0
- pos_table: float32 [2048, 512], P('tp')
- w_conv1: bfloat16 [3, 80, 512], replicated
- b_conv1: bfloat16 [512], replicated
- w_conv2: bfloat16 [3, 512, 512], replicated
- b_conv2: bfloat16 [512], replicated
- ln1_gain: bfloat16 [512], replicated
- ln1_bias: bfloat16 [512], replicated
- w_query: bfloat16 [512, 512], P(None, 'tp')
- b_query: bfloat16 [512], P('tp')
- w_key: bfloat16 [512, 512], P(None, 'tp')
- w_value: bfloat16 [512, 512], P(None, 'tp')
- b_value: bfloat16 [512], P('tp')
- w_out: bfloat16 [512, 512], P('tp')
- b_out: bfloat16 [512], replicated
- ln2_gain: bfloat16 [512], replicated
- ln2_bias: bfloat16 [512], replicated
- w_fc1: bfloat16 [512, 2048], P(None, 'tp')
- b_fc1: bfloat16 [2048], P('tp')
- w_fc2: bfloat16 [2048, 512], P('tp')
- b_fc2: bfloat16 [512], replicated
- grad_y: bfloat16 [8, 2048, 512], P('dp', 'tp'), parts along dimension 0
Outputs:
- output 1: bfloat16 [8, 2048, 512], P('dp', 'tp'), parts along dimension 0
- output 2: bfloat16 [8, 4096, 80], P('dp', 'tp'), parts along dimension 0
- output 3: float32 [12, 80, 512], P('dp'), parts along dimension 0
- output 4: float32 [2048], P('dp'), parts along dimension 0
- output 5: float32 [12, 512, 512], P('dp'), parts along dimension 0
- output 6: float32 [2048], P('dp'), parts along dimension 0
- output 7: float32 [2048], P('dp'), parts along dimension 0
- output 8: float32 [2048], P('dp'), parts along dimension 0
- output 9: float32 [2048, 512], P('dp', 'tp'), parts along dimension 0
- output 10: float32 [2048], P(('dp', 'tp')), parts along dimension 0
- output 11: float32 [2048, 512], P('dp', 'tp'), parts along dimension 0
- output 12: float32 [2048, 512], P('dp', 'tp'), parts along dimension 0
- output 13: float32 [2048], P(('dp', 'tp')), parts along dimension 0
- output 14: float32 [2048, 512], P(('dp', 'tp')), parts along dimension 0
- output 15: float32 [2048], P('dp'), parts along dimension 0
- output 16: float32 [2048], P('dp'), parts along dimension 0
- output 17: float32 [2048], P('dp'), parts along dimension 0
- output 18: float32 [2048, 2048], P('dp', 'tp'), parts along dimension 0
- output 19: float32 [8192], P(('dp', 'tp')), parts along dimension 0
- output 20: float32 [8192, 512], P(('dp', 'tp')), parts along dimension 0
- output 21: float32 [2048], P('dp'), parts along dimension 0
There are 4 independent parts. A program takes and returns all parts, laid end to end along the dimension named above; an argument that names none is the same for every part.
All inputs are finite; a program needn't handle non-finite values.
Results may differ from a plain program's by a relative error of at most 0.02.
Values are sent between devices in bfloat16 or wider.
A program may use at most 768 MiB of HBM per device.

v0:
```python
import functools
import jax
import jax.numpy as jnp
from jax import lax
from jax.sharding import PartitionSpec as P

HEAD_DIM = 64
LN_EPS = 1e-5


def gelu_exact(values):
    return jax.nn.gelu(values, approximate=False)


def contract(pattern, lhs, rhs):
    return jnp.einsum(pattern, lhs, rhs, preferred_element_type=jnp.float32)


def norm_f32(x_f32, gain_vec, shift_vec):
    row_mean = jnp.mean(x_f32, axis=-1, keepdims=True)
    centred = x_f32 - row_mean
    row_var = jnp.mean(centred * centred, axis=-1, keepdims=True)
    return centred * lax.rsqrt(row_var + LN_EPS) * gain_vec + shift_vec


def norm_with_grad(values, gain_vec, shift_vec):
    normed, norm_back = jax.vjp(norm_f32, values.astype(jnp.float32), gain_vec.astype(jnp.float32),
                                shift_vec.astype(jnp.float32))
    return normed.astype(jnp.bfloat16), norm_back


def neighbour_rows(gathered, offset, my_rank, group_size):
    source = my_rank + offset
    picked = lax.dynamic_index_in_dim(gathered, jnp.clip(source, 0, group_size - 1), 0, keepdims=False)
    inside = (source >= 0) & (source < group_size)
    return jnp.where(inside, picked, jnp.zeros_like(picked))


def device_step(mel_in, pos_table, w_conv1, b_conv1, w_conv2, b_conv2, ln1_gain, ln1_bias, w_query, b_query,
                w_key, w_value, b_value, w_out, b_out, ln2_gain, ln2_bias, w_fc1, b_fc1, w_fc2, b_fc2, grad_y,
                group_size):
    my_rank = lax.axis_index('tp')
    n_batch, mel_len = mel_in.shape[:2]
    frames = mel_len // 2
    model_width = w_conv2.shape[-1]
    local_width = w_query.shape[-1]
    scale_qk = HEAD_DIM ** -0.5

    mel_edges = lax.all_gather(jnp.concatenate([mel_in[:, :1], mel_in[:, -2:]], axis=1), 'tp')
    mel_ext = jnp.concatenate([neighbour_rows(mel_edges, -1, my_rank, group_size)[:, 1:], mel_in,
                               neighbour_rows(mel_edges, 1, my_rank, group_size)[:, :1]], axis=1)
    windows = jnp.stack([mel_ext[:, tap_idx:tap_idx + mel_len + 1] for tap_idx in range(3)], axis=2)
    h1_pre = contract('bltm,tmd->bld', windows, w_conv1) + b_conv1.astype(jnp.float32)
    h1_act, gelu_back_one = jax.vjp(gelu_exact, h1_pre)
    keep_first = (jnp.arange(mel_len + 1) > 0) | (my_rank > 0)
    h1_ext = jnp.where(keep_first[None, :, None], h1_act, 0.0).astype(jnp.bfloat16)
    h1_pairs = h1_ext[:, :mel_len].reshape(n_batch, frames, 2, model_width)
    h1_after = h1_ext[:, 1:].reshape(n_batch, frames, 2, model_width)[:, :, 1]
    h2_pre = (contract('bfsd,sde->bfe', h1_pairs, w_conv2[:2]) + contract('bfd,de->bfe', h1_after, w_conv2[2])
              + b_conv2.astype(jnp.float32))
    h2_act, gelu_back_two = jax.vjp(gelu_exact, h2_pre)
    x_embed = (h2_act + pos_table).astype(jnp.bfloat16)

    norm_one, norm_one_back = norm_with_grad(x_embed, ln1_gain, ln1_bias)
    norm_one_all = lax.all_gather(norm_one, 'tp', axis=1, tiled=True)
    seq_len = norm_one_all.shape[1]
    head_shape = (n_batch, seq_len, local_width // HEAD_DIM, HEAD_DIM)
    flat_shape = (n_batch, seq_len, local_width)
    q_heads = (contract('btd,dc->btc', norm_one_all, w_query) + b_query.astype(jnp.float32)).astype(jnp.bfloat16).reshape(head_shape)
    k_heads = contract('btd,dc->btc', norm_one_all, w_key).astype(jnp.bfloat16).reshape(head_shape)
    v_heads = (contract('btd,dc->btc', norm_one_all, w_value) + b_value.astype(jnp.float32)).astype(jnp.bfloat16).reshape(head_shape)
    attn_probs = jax.nn.softmax(contract('bqhe,bkhe->bhqk', q_heads, k_heads) * scale_qk, axis=-1)
    probs_low = attn_probs.astype(jnp.bfloat16)
    attn_flat = contract('bhqk,bkhe->bqhe', probs_low, v_heads).astype(jnp.bfloat16).reshape(flat_shape)
    attn_sum = lax.psum_scatter(contract('btc,cd->btd', attn_flat, w_out).astype(jnp.bfloat16), 'tp',
                                scatter_dimension=1, tiled=True)
    x_mid = (x_embed.astype(jnp.float32) + attn_sum.astype(jnp.float32) + b_out.astype(jnp.float32)).astype(jnp.bfloat16)

    norm_two, norm_two_back = norm_with_grad(x_mid, ln2_gain, ln2_bias)
    norm_two_all = lax.all_gather(norm_two, 'tp', axis=1, tiled=True)
    fc_act, gelu_back_fc = jax.vjp(gelu_exact, contract('btd,df->btf', norm_two_all, w_fc1) + b_fc1.astype(jnp.float32))
    fc_hidden = fc_act.astype(jnp.bfloat16)
    mlp_sum = lax.psum_scatter(contract('btf,fd->btd', fc_hidden, w_fc2).astype(jnp.bfloat16), 'tp',
                               scatter_dimension=1, tiled=True)
    y_out = (x_mid.astype(jnp.float32) + mlp_sum.astype(jnp.float32) + b_fc2.astype(jnp.float32)).astype(jnp.bfloat16)

    grad_f32 = grad_y.astype(jnp.float32)
    d_b_fc2 = jnp.sum(grad_f32, axis=(0, 1))
    grad_all = lax.all_gather(grad_y, 'tp', axis=1, tiled=True)
    d_w_fc2 = contract('btf,btd->fd', fc_hidden, grad_all)
    d_fc_pre = gelu_back_fc(contract('btd,fd->btf', grad_all, w_fc2))[0]
    d_b_fc1 = jnp.sum(d_fc_pre, axis=(0, 1))
    d_fc_low = d_fc_pre.astype(jnp.bfloat16)
    d_w_fc1 = contract('btd,btf->df', norm_two_all, d_fc_low)
    d_norm_two = lax.psum_scatter(contract('btf,df->btd', d_fc_low, w_fc1).astype(jnp.bfloat16), 'tp',
                                  scatter_dimension=1, tiled=True)
    d_mid_norm, d_ln2_gain, d_ln2_bias = norm_two_back(d_norm_two.astype(jnp.float32))
    d_mid = grad_f32 + d_mid_norm
    d_b_out = jnp.sum(d_mid, axis=(0, 1))
    d_mid_all = lax.all_gather(d_mid.astype(jnp.bfloat16), 'tp', axis=1, tiled=True)
    d_w_out = contract('btc,btd->cd', attn_flat, d_mid_all)
    d_attn = contract('btd,cd->btc', d_mid_all, w_out).astype(jnp.bfloat16).reshape(head_shape)
    d_probs = contract('bqhe,bkhe->bhqk', d_attn, v_heads)
    d_value = contract('bhqk,bqhe->bkhe', probs_low, d_attn).reshape(flat_shape)
    d_scores = attn_probs * (d_probs - jnp.sum(d_probs * attn_probs, axis=-1, keepdims=True))
    d_scores_low = (d_scores * scale_qk).astype(jnp.bfloat16)
    d_query = contract('bhqk,bkhe->bqhe', d_scores_low, k_heads).reshape(flat_shape)
    d_key = contract('bhqk,bqhe->bkhe', d_scores_low, q_heads).reshape(flat_shape)
    d_b_query = jnp.sum(d_query, axis=(0, 1))
    d_b_value = jnp.sum(d_value, axis=(0, 1))
    d_query_low = d_query.astype(jnp.bfloat16)
    d_key_low = d_key.astype(jnp.bfloat16)
    d_value_low = d_value.astype(jnp.bfloat16)
    d_w_query = contract('btd,btc->dc', norm_one_all, d_query_low)
    d_w_key = contract('btd,btc->dc', norm_one_all, d_key_low)
    d_w_value = contract('btd,btc->dc', norm_one_all, d_value_low)
    d_norm_one_part = (contract('btc,dc->btd', d_query_low, w_query) + contract('btc,dc->btd', d_key_low, w_key)
                       + contract('btc,dc->btd', d_value_low, w_value))
    d_norm_one = lax.psum_scatter(d_norm_one_part.astype(jnp.bfloat16), 'tp', scatter_dimension=1, tiled=True)
    d_embed_norm, d_ln1_gain, d_ln1_bias = norm_one_back(d_norm_one.astype(jnp.float32))
    d_embed = d_mid + d_embed_norm

    d_h2_pre = gelu_back_two(d_embed)[0]
    d_b_conv2 = jnp.sum(d_h2_pre, axis=(0, 1))
    d_h2_low = d_h2_pre.astype(jnp.bfloat16)
    d_w_conv2 = jnp.concatenate([contract('bfsd,bfe->sde', h1_pairs, d_h2_low),
                                 contract('bfd,bfe->de', h1_after, d_h2_low)[None]], axis=0)
    d_taps = contract('bfe,tde->bftd', d_h2_low, w_conv2)
    tap_edges = lax.all_gather(d_taps[:, 0, 0], 'tp')
    from_right = neighbour_rows(tap_edges, 1, my_rank, group_size)
    odd_frames = d_taps[:, :, 2] + jnp.concatenate([d_taps[:, 1:, 0], from_right[:, None]], axis=1)
    d_h1 = jnp.stack([d_taps[:, :, 1], odd_frames], axis=2).reshape(n_batch, mel_len, model_width)
    d_h1_pre = gelu_back_one(jnp.pad(d_h1, ((0, 0), (1, 0), (0, 0))))[0][:, 1:]
    d_b_conv1 = jnp.sum(d_h1_pre, axis=(0, 1))
    d_h1_low = d_h1_pre.astype(jnp.bfloat16)
    d_w_conv1 = contract('bltm,bld->tmd', windows[:, 1:], d_h1_low)
    d_windows = contract('bld,tmd->bltm', d_h1_low, w_conv1)
    mel_tap_edges = lax.all_gather(jnp.stack([d_windows[:, 0, 0], d_windows[:, -1, 2]], axis=1), 'tp')
    from_right_mel = neighbour_rows(mel_tap_edges, 1, my_rank, group_size)[:, 0]
    from_left_mel = neighbour_rows(mel_tap_edges, -1, my_rank, group_size)[:, 1]
    d_mel = (d_windows[:, :, 1]
             + jnp.concatenate([d_windows[:, 1:, 0], from_right_mel[:, None]], axis=1)
             + jnp.concatenate([from_left_mel[:, None], d_windows[:, :-1, 2]], axis=1)).astype(jnp.bfloat16)

    summed = lax.psum((d_w_conv1, d_b_conv1, d_w_conv2, d_b_conv2, d_ln1_gain, d_ln1_bias, d_b_out,
                       d_ln2_gain, d_ln2_bias, d_b_fc2), 'tp')
    return (y_out, d_mel, summed[0], summed[1], summed[2], summed[3], summed[4], summed[5], d_w_query,
            d_b_query, d_w_key, d_w_value, d_b_value, d_w_out, summed[6], summed[7], summed[8], d_w_fc1,
            d_b_fc1, d_w_fc2, summed[9])


def solution(mesh):
    group_size = mesh.shape['tp']
    in_specs = (P('dp', 'tp', None), P('tp', None), P(), P(), P(), P(), P(), P(),
                P(None, 'tp'), P('tp'), P(None, 'tp'), P(None, 'tp'), P('tp'), P('tp', None), P(), P(), P(),
                P(None, 'tp'), P('tp'), P('tp', None), P(), P('dp', 'tp', None))
    out_specs = (P('dp', 'tp', None), P('dp', 'tp', None), P('dp', None, None), P('dp'), P('dp', None, None),
                 P('dp'), P('dp'), P('dp'), P('dp', 'tp'), P(('dp', 'tp')), P('dp', 'tp'), P('dp', 'tp'),
                 P(('dp', 'tp')), P(('dp', 'tp'), None), P('dp'), P('dp'), P('dp'), P('dp', 'tp'),
                 P(('dp', 'tp')), P(('dp', 'tp'), None), P('dp'))
    local_step = functools.partial(device_step, group_size=group_size)
    return jax.shard_map(local_step, mesh=mesh, in_specs=in_specs, out_specs=out_specs, check_vma=False)
```

profile of v0, /device:TPU:81, one launch (start us, length us, event | category | flops | bytes accessed | tf_op | source)
XLA Modules:
  0.0 601.4 jit_solution(6314288282949971292)
XLA Ops:
  11.9 14.8 %all-gather = bf16[16,3,80]{2,1,0:T(4,128)(2,1)S(1)} all-gather(bf16[2,3,80]{2,1,0:T(4,128)(2,1)S(1)} %pad_maximum_fusion.3), channel_id=2, replica_groups=mesh['dp'=4,'tp'=8] {'tp'}, dimensions={0}, use_global_device_ids=true | all-gather | bytes 8640 | tf_op jit(solution)/shard_map/all_gather | solution.py:49
  28.4 8.0 %select_convert_fusion = (bf16[2,513,512]{2,1,0:T(8,128)(2,1)S(1)}, f32[2,513,512]{2,1,0:T(8,128)}, f32[2,513,512]{2,1,0:T(8,128)}, f32[2,513,512]{2,1,0:T(8,128)}) fusion(pred[513]{0:T(1024)(128)(4,1)S(1)} %fusion.149, f32[512]{0:T(512)S(1)} %convert_element_type.171, bf16[3,80,512]{2,1,0:T(8,128)(2,1)} %param.24, ...), kind=kOutput, calls=%fused_computation.56 | convolution fusion | flops 287838144 | bytes 8095169 | tf_op jit(solution)/shard_map/bltm,tmd->bld/dot_general | solution.py:16
  39.8 1.9 convolution_bitcast_fusion.2
  41.8 5.3 convert_reduce_fusion.3
  48.9 31.1 %all-gather.8.cloned.1.call-done = bf16[2,2048,512]{2,1,0:T(8,128)(2,1)} async-done(((bf16[2,256,512]{2,1,0:T(8,128)(2,1)}), bf16[2,2048,512]{2,1,0:T(8,128)(2,1)}) %all-gather.8.cloned.1.call-update) | async-done | bytes 4194320 | tf_op jit(solution)/shard_map/all_gather | solution.py:65
  80.0 3.7 convolution_convert_fusion.4
  85.2 15.2 %fusion.174 = (f32[2,2048]{1,0:T(2,128)S(1)}, f32[2,2048,2048]{1,2,0:T(8,128)}) fusion(bf16[2,2048,64]{1,2,0:T(8,128)(2,1)S(1)} %fusion.31, bf16[2,2048,64]{1,2,0:T(8,128)(2,1)S(1)} %convolution_convert_fusion.4), kind=kOutput, calls=%fused_computation.261 | convolution fusion | flops 1098909696 | bytes 34619392 | tf_op jit(solution)/shard_map/sub | solution.py:72
  100.4 3.6 fusion.30
  104.0 12.2 %fusion.38 = bf16[2,2048,64]{1,2,0:T(8,128)(2,1)S(1)} fusion(bf16[2,2048,64]{1,2,0:T(8,128)(2,1)S(1)} %fusion.30, f32[2,2048,2048]{1,2,0:T(8,128)} %get-tuple-element.76, f32[2,2048]{1,0:T(2,128)S(1)} %get-tuple-element.75), kind=kOutput, calls=%fused_computation.53 | convolution fusion | flops 1090781184 | bytes 34619392 | tf_op jit(solution)/shard_map/bhqk,bkhe->bqhe/dot_general | solution.py:16
  117.1 3.4 convolution_convert_fusion.2
  120.6 31.5 %reduce-scatter.5.cloned.1.call-done = bf16[2,256,512]{2,1,0:T(8,128)(2,1)} async-done(((bf16[2,2048,512]{2,1,0:T(8,128)(2,1)}), bf16[2,256,512]{2,1,0:T(8,128)(2,1)}) %reduce-scatter.5.cloned.1.call-update) | async-done | bytes 524304 | tf_op jit(solution)/shard_map/reduce_scatter | solution.py:75
  156.1 29.9 %all-gather.10.cloned.1.call-done = bf16[2,2048,512]{2,1,0:T(8,128)(2,1)} async-done(((bf16[2,256,512]{2,1,0:T(8,128)(2,1)}), bf16[2,2048,512]{2,1,0:T(8,128)(2,1)}) %all-gather.10.cloned.1.call-update) | async-done | bytes 4194320 | tf_op jit(solution)/shard_map/all_gather | solution.py:80
  185.9 4.3 fusion.99
  190.2 2.0 copy-done.23
  192.2 10.7 %multiply_convert_fusion.1 = (bf16[2,2048,256]{2,1,0:T(8,128)(2,1)S(1)}, f32[2,2048,256]{2,1,0:T(8,128)}) fusion(f32[2,2048,256]{2,1,0:T(8,128)S(1)} %get-tuple-element.77, f32[256]{0:T(256)S(1)} %convert_element_type.196, u8[2048,256]{1,0:T(8,128)(4,1)S(1)} %get-tuple-element.22, u8[2048,256]{1,0:T(8,128)(4,1)S(1)} %get-tuple-element.21), kind=kLoop, calls=%fused_computation.26 | loop fusion | flops 74448896 | bytes 11535360 | tf_op jit(solution)/shard_map/convert_element_type | solution.py:82
  202.9 13.1 %all-gather.12.cloned.1.call-done = bf16[2,2048,512]{2,1,0:T(8,128)(2,1)} async-done(((bf16[2,256,512]{2,1,0:T(8,128)(2,1)}), bf16[2,2048,512]{2,1,0:T(8,128)(2,1)}) %all-gather.12.cloned.1.call-update) | async-done | bytes 4194320 | tf_op jit(solution)/shard_map/all_gather | solution.py:89
  216.0 7.6 %fusion.179 = (f32[256]{0:T(256)}, bf16[2,2048,256]{2,1,0:T(8,128)(2,1)S(1)}) fusion(f32[2,2048,256]{2,1,0:T(8,128)} %get-tuple-element.49, bf16[2,2048,512]{2,1,0:T(8,128)(2,1)} %all-gather.12.cloned.1.call-done, bf16[256,512]{1,0:T(8,128)(2,1)} %param.41, f32[2,2048,256]{2,1,0:T(8,128)} %copy-done.23, f32[256]{0:T(256)S(1)} %convert_element_type.196), kind=kOutput, calls=%fused_computation.264 | convolution fusion | flops 1090518784 | bytes 14944256 | tf_op jit(solution)/shard_map/btd,fd->btf/dot_general | solution.py:16
  225.0 3.4 convolution_convert_fusion
  229.3 3.2 convolution_convert_fusion.1
  232.7 27.3 %reduce-scatter.9.cloned.1.call-done = bf16[2,256,512]{2,1,0:T(8,128)(2,1)} async-done(((bf16[2,2048,512]{2,1,0:T(8,128)(2,1)}), bf16[2,256,512]{2,1,0:T(8,128)(2,1)}) %reduce-scatter.9.cloned.1.call-update) | async-done | bytes 524304 | tf_op jit(solution)/shard_map/reduce_scatter | solution.py:95
  260.1 2.0 convert_reduce_fusion.1
  263.7 32.3 %reduce-scatter.7.cloned.1.call-done = bf16[2,256,512]{2,1,0:T(8,128)(2,1)} async-done(((bf16[2,2048,512]{2,1,0:T(8,128)(2,1)}), bf16[2,256,512]{2,1,0:T(8,128)(2,1)}) %reduce-scatter.7.cloned.1.call-update) | async-done | bytes 524304 | tf_op jit(solution)/shard_map/reduce_scatter | solution.py:83
  296.0 3.6 fusion.82
  299.9 30.8 %all-gather.14.cloned.1.call-done = bf16[2,2048,512]{2,1,0:T(8,128)(2,1)} async-done(((bf16[2,256,512]{2,1,0:T(8,128)(2,1)}), bf16[2,2048,512]{2,1,0:T(8,128)(2,1)}) %all-gather.14.cloned.1.call-update) | async-done | bytes 4194320 | tf_op jit(solution)/shard_map/all_gather | solution.py:100
  330.7 3.6 convolution_convert_fusion.3
  334.3 13.9 %fusion.178 = (f32[64]{0:T(128)}, bf16[2,64,2048]{2,1,0:T(8,128)(2,1)S(1)}) fusion(bf16[2,2048,64]{1,2,0:T(8,128)(2,1)S(1)} %convolution_convert_fusion.3, f32[2,2048,2048]{1,2,0:T(8,128)} %get-tuple-element.76, f32[2,2048]{1,0:T(2,128)S(1)} %get-tuple-element.75), kind=kOutput, calls=%fused_computation.263 | convolution fusion | flops 1091043328 | bytes 34619648 | tf_op jit(solution)/shard_map/bhqk,bqhe->bkhe/dot_general | solution.py:16
  348.2 13.1 %fusion.180 = f32[2,2048,2048]{1,2,0:T(8,128)} fusion(bf16[2,2048,64]{1,2,0:T(8,128)(2,1)S(1)} %convolution_convert_fusion.3, bf16[2,2048,64]{1,2,0:T(8,128)(2,1)S(1)} %fusion.30), kind=kOutput, calls=%fused_computation.265 | convolution fusion | flops 1073741824 | bytes 34603008 | tf_op jit(solution)/shard_map/bqhe,bkhe->bhqk/dot_general | solution.py:16
  361.3 41.8 %fusion.35 = bf16[2,2048,64]{1,2,0:T(8,128)(2,1)S(1)} fusion(bf16[2,2048,64]{1,2,0:T(8,128)(2,1)S(1)} %copy-done.36, f32[2,2048,2048]{1,2,0:T(8,128)} %fusion.180, f32[2,2048,2048]{1,2,0:T(8,128)} %get-tuple-element.76, f32[2,2048]{1,0:T(2,128)S(1)} %get-tuple-element.75), kind=kOutput, calls=%fused_computation.52 | convolution fusion | flops 1132730368 | bytes 68173824 | tf_op jit(solution)/shard_map/bhqk,bqhe->bkhe/dot_general | solution.py:16
  403.2 42.9 %fusion.175 = (f32[64]{0:T(128)}, bf16[2,64,2048]{2,1,0:T(8,128)(2,1)S(1)}) fusion(bf16[2,2048,64]{1,2,0:T(8,128)(2,1)S(1)} %copy-done.34, f32[2,2048,2048]{1,2,0:T(8,128)} %fusion.180, f32[2,2048,2048]{1,2,0:T(8,128)} %get-tuple-element.76, f32[2,2048]{1,0:T(2,128)S(1)} %get-tuple-element.75), kind=kOutput, calls=%fused_computation.262 | convolution fusion | flops 1132992512 | bytes 68174080 | tf_op jit(solution)/shard_map/bhqk,bkhe->bqhe/dot_general | solution.py:16
  448.7 3.2 add_convert_fusion
  453.6 4.4 convolution_bitcast_fusion.3
  458.0 2.1 convolution_bitcast_fusion.4
  462.0 21.6 %reduce-scatter.11.cloned.1.call-done = bf16[2,256,512]{2,1,0:T(8,128)(2,1)} async-done(((bf16[2,2048,512]{2,1,0:T(8,128)(2,1)}), bf16[2,256,512]{2,1,0:T(8,128)(2,1)}) %reduce-scatter.11.cloned.1.call-update) | async-done | bytes 524304 | tf_op jit(solution)/shard_map/reduce_scatter | solution.py:119
  485.2 1.8 fusion.83
  487.0 2.7 fusion.164
  491.2 2.1 convolution_bitcast_fusion
  495.4 16.3 %all-gather.1 = f32[16,1,1,512]{3,2,1,0:T(1,128)S(1)} all-gather(f32[2,1,1,512]{3,2,1,0:T(1,128)S(1)} %slice_bitcast_fusion.3), channel_id=3, replica_groups=mesh['dp'=4,'tp'=8] {'tp'}, dimensions={0}, use_global_device_ids=true | all-gather | bytes 36864 | tf_op jit(solution)/shard_map/all_gather | solution.py:129
  511.9 1.6 fusion.172
  513.6 3.0 copy.126
  516.6 2.7 reshape.232
  519.4 4.0 fusion.165
  524.7 2.0 pad_maximum_fusion
  526.8 3.8 convolution_bitcast_fusion.6
  534.3 12.9 %all-gather.2 = f32[16,2,80]{2,1,0:T(2,128)S(1)} all-gather(f32[2,2,80]{2,1,0:T(2,128)S(1)} %copy.129), channel_id=4, replica_groups=mesh['dp'=4,'tp'=8] {'tp'}, dimensions={0}, use_global_device_ids=true | all-gather | bytes 11520 | tf_op jit(solution)/shard_map/all_gather | solution.py:138
  547.7 20.5 %all-reduce.1 = (f32[512]{0:T(512)}, f32[512]{0:T(512)}, f32[512]{0:T(512)}, f32[512]{0:T(512)}, f32[512]{0:T(512)}, /*index=5*/f32[512]{0:T(512)}, f32[512]{0:T(512)}, f32[512]{0:T(512)}) all-reduce(f32[512]{0:T(512)S(1)} %get-tuple-element.46, f32[512]{0:T(512)S(1)} %get-tuple-element.44, ...), channel_id=1, replica_groups=mesh['dp'=4,'tp'=8] {'tp'}, use_global_device_ids=true, to_apply=%region_17.18 | all-reduce | flops 4096 | bytes 32768 | tf_op jit(solution)/shard_map/psum | solution.py:145
  569.2 19.6 %all-reduce.5.cloned.1.call-done = (f32[3,80,512]{2,1,0:T(8,128)}, f32[3,512,512]{2,1,0:T(8,128)}) async-done(((f32[3,80,512]{2,1,0:T(8,128)}, f32[3,512,512]{2,1,0:T(8,128)}), (f32[3,80,512]{2,1,0:T(8,128)}, f32[3,512,512]{2,1,0:T(8,128)})) %all-reduce.5.cloned.1.call-update) | async-done | bytes 3637264 | tf_op jit(solution)/shard_map/psum | solution.py:145
  588.8 1.8 copy.166
  590.6 3.9 copy.167
  (244 shorter events, 39.7 us)
Async XLA Ops:
  7.2 178.7 %copy-start = (bf16[512,256]{1,0:T(8,128)(2,1)S(1)}, bf16[512,256]{1,0:T(8,128)(2,1)}, u32[]{:S(2)}) copy-start(bf16[512,256]{1,0:T(8,128)(2,1)} %param.39) | copy-start | bytes 786436
  7.2 72.8 %all-gather.8.cloned.1.call-start = ((), (), s32[]{:S(2)}) async-start(), calls=%async_computation.4 | async-start | bytes 4718592 | tf_op jit(solution)/shard_map/all_gather | solution.py:65
  9.6 37.8 %copy-start.58 = (f32[512]{0:T(512)}, f32[512]{0:T(512)S(1)}, u32[]{:S(2)}) copy-start(f32[512]{0:T(512)S(1)} %convert_element_type.176) | copy-start | bytes 6148
  41.7 38.2 %copy-start.37 = (bf16[512,64]{0,1:T(8,128)(2,1)S(1)}, bf16[512,64]{0,1:T(8,128)(2,1)}, u32[]{:S(2)}) copy-start(bf16[512,64]{0,1:T(8,128)(2,1)} %param.32) | copy-start | bytes 196612
  47.1 105.1 %copy-start.8 = (bf16[2,256,512]{2,1,0:T(8,128)(2,1)}, bf16[2,256,512]{2,1,0:T(8,128)(2,1)S(1)}, u32[]{:S(2)}) copy-start(bf16[2,256,512]{2,1,0:T(8,128)(2,1)S(1)} %get-tuple-element.53) | copy-start | bytes 1572868
  47.1 36.6 %copy-start.41 = (bf16[512,64]{0,1:T(8,128)(2,1)S(1)}, bf16[512,64]{0,1:T(8,128)(2,1)}, u32[]{:S(2)}) copy-start(bf16[512,64]{0,1:T(8,128)(2,1)} %param.30) | copy-start | bytes 196612
  47.1 32.9 %copy-start.54 = (f32[2,256]{1,0:T(2,128)}, f32[2,256]{1,0:T(2,128)S(1)}, u32[]{:S(2)}) copy-start(f32[2,256]{1,0:T(2,128)S(1)} %broadcast_multiply_fusion.1) | copy-start | bytes 6148
  47.4 32.6 %copy-start.66 = (f32[2,256]{1,0:T(2,128)}, f32[2,256]{1,0:T(2,128)S(1)}, u32[]{:S(2)}) copy-start(f32[2,256]{1,0:T(2,128)S(1)} %fusion.74) | copy-start | bytes 6148
  47.5 32.5 %copy-start.62 = (f32[2,256]{1,0:T(2,128)}, f32[2,256]{1,0:T(2,128)S(1)}, u32[]{:S(2)}) copy-start(f32[2,256]{1,0:T(2,128)S(1)} %fusion.150) | copy-start | bytes 6148
  48.6 103.6 %reduce-scatter.5.cloned.1.call-start = ((), (), s32[]{:S(2)}) async-start(), calls=%async_computation.5 | async-start | bytes 4718592 | tf_op jit(solution)/shard_map/reduce_scatter | solution.py:75
  83.7 16.7 %copy-start.33 = (bf16[2,2048,64]{1,2,0:T(8,128)(2,1)}, bf16[2,2048,64]{1,2,0:T(8,128)(2,1)S(1)}, u32[]{:S(2)}) copy-start(bf16[2,2048,64]{1,2,0:T(8,128)(2,1)S(1)} %convolution_convert_fusion.4) | copy-start | bytes 1572868
  120.4 35.6 %copy-start.80 = (bf16[256]{0:T(256)(128)(2,1)S(1)}, bf16[256]{0:T(256)(128)(2,1)}, u32[]{:S(2)}) copy-start(bf16[256]{0:T(256)(128)(2,1)} %param.40) | copy-start | bytes 1540
  120.5 65.4 %all-gather.10.cloned.1.call-start = ((), (), s32[]{:S(2)}) async-start(), calls=%async_computation.6 | async-start | bytes 4718592 | tf_op jit(solution)/shard_map/all_gather | solution.py:80
  120.6 175.4 %copy-start.56 = (f32[512]{0:T(512)}, f32[512]{0:T(512)S(1)}, u32[]{:S(2)}) copy-start(f32[512]{0:T(512)S(1)} %convert_element_type.193) | copy-start | bytes 6148
  153.5 142.6 %copy-start.4 = (bf16[2,256,512]{2,1,0:T(8,128)(2,1)}, bf16[2,256,512]{2,1,0:T(8,128)(2,1)S(1)}, u32[]{:S(2)}) copy-start(bf16[2,256,512]{2,1,0:T(8,128)(2,1)S(1)} %get-tuple-element.51) | copy-start | bytes 1572868
  153.5 142.5 %copy-start.52 = (f32[2,256]{1,0:T(2,128)}, f32[2,256]{1,0:T(2,128)S(1)}, u32[]{:S(2)}) copy-start(f32[2,256]{1,0:T(2,128)S(1)} %broadcast_multiply_fusion) | copy-start | bytes 6148
  153.8 142.2 %copy-start.60 = (f32[2,256]{1,0:T(2,128)}, f32[2,256]{1,0:T(2,128)S(1)}, u32[]{:S(2)}) copy-start(f32[2,256]{1,0:T(2,128)S(1)} %fusion.151) | copy-start | bytes 6148
  154.9 61.1 %all-gather.12.cloned.1.call-start = ((), (), s32[]{:S(2)}) async-start(), calls=%async_computation.8 | async-start | bytes 4718592 | tf_op jit(solution)/shard_map/all_gather | solution.py:89
  155.6 104.5 %reduce-scatter.9.cloned.1.call-start = ((), (), s32[]{:S(2)}) async-start(), calls=%async_computation.9 | async-start | bytes 4718592 | tf_op jit(solution)/shard_map/reduce_scatter | solution.py:95
  202.9 25.6 %copy-start.6 = (bf16[2,2048,256]{2,1,0:T(8,128)(2,1)}, bf16[2,2048,256]{2,1,0:T(8,128)(2,1)S(1)}, u32[]{:S(2)}) copy-start(bf16[2,2048,256]{2,1,0:T(8,128)(2,1)S(1)} %get-tuple-element.48) | copy-start | bytes 6291460
  228.5 67.6 %reduce-scatter.7.cloned.1.call-start = ((), (), s32[]{:S(2)}) async-start(), calls=%async_computation.7 | async-start | bytes 4718592 | tf_op jit(solution)/shard_map/reduce_scatter | solution.py:83
  232.6 63.4 %copy-start.21 = (bf16[2,256,512]{2,1,0:T(8,128)(2,1)S(1)}, bf16[2,256,512]{2,1,0:T(8,128)(2,1)}, u32[]{:S(2)}) copy-start(bf16[2,256,512]{2,1,0:T(8,128)(2,1)} %param.43) | copy-start | bytes 1572868
  232.7 98.1 %all-gather.14.cloned.1.call-start = ((), (), s32[]{:S(2)}) async-start(), calls=%async_computation.10 | async-start | bytes 4718592 | tf_op jit(solution)/shard_map/all_gather | solution.py:100
  262.1 72.2 %copy-start.64 = (f32[2,256]{1,0:T(2,128)}, f32[2,256]{1,0:T(2,128)S(1)}, u32[]{:S(2)}) copy-start(f32[2,256]{1,0:T(2,128)S(1)} %multiply_multiply_fusion.16) | copy-start | bytes 6148
  263.7 70.7 %copy-start.68 = (f32[2,256]{1,0:T(2,128)}, f32[2,256]{1,0:T(2,128)S(1)}, u32[]{:S(2)}) copy-start(f32[2,256]{1,0:T(2,128)S(1)} %negate_multiply_fusion.4) | copy-start | bytes 6148
  299.6 184.0 %reduce-scatter.11.cloned.1.call-start = ((), (), s32[]{:S(2)}) async-start(), calls=%async_computation.11 | async-start | bytes 4718592 | tf_op jit(solution)/shard_map/reduce_scatter | solution.py:119
  348.2 100.5 %copy-start.30 = (bf16[2,64,2048]{2,1,0:T(8,128)(2,1)}, bf16[2,64,2048]{2,1,0:T(8,128)(2,1)S(1)}, u32[]{:S(2)}) copy-start(bf16[2,64,2048]{2,1,0:T(8,128)(2,1)S(1)} %get-tuple-element.81) | copy-start | bytes 1572868
  361.3 41.8 %copy-start.34 = (bf16[2,2048,64]{1,2,0:T(8,128)(2,1)S(1)}, bf16[2,2048,64]{1,2,0:T(8,128)(2,1)}, u32[]{:S(2)}) copy-start(bf16[2,2048,64]{1,2,0:T(8,128)(2,1)} %copy-done.33) | copy-start | bytes 1572868
  403.1 43.0 %copy-start.15 = (bf16[2,2048,64]{1,2,0:T(8,128)(2,1)}, bf16[2,2048,64]{1,2,0:T(8,128)(2,1)S(1)}, u32[]{:S(2)}) copy-start(bf16[2,2048,64]{1,2,0:T(8,128)(2,1)S(1)} %fusion.35) | copy-start | bytes 1572868
  403.1 43.0 %copy-start.38 = (bf16[512,64]{0,1:T(8,128)(2,1)S(1)}, bf16[512,64]{0,1:T(8,128)(2,1)}, u32[]{:S(2)}) copy-start(bf16[512,64]{0,1:T(8,128)(2,1)} %param.32) | copy-start | bytes 196612
  452.0 136.8 %all-reduce.5.cloned.1.call-start = ((), (), s32[]{:S(2)}) async-start(), calls=%async_computation.12 | async-start | bytes 7274496 | tf_op jit(solution)/shard_map/psum | solution.py:145
  458.0 25.7 %copy-start.9 = (bf16[2,256,512]{2,1,0:T(8,128)(2,1)S(1)}, bf16[2,256,512]{2,1,0:T(8,128)(2,1)}, u32[]{:S(2)}) copy-start(bf16[2,256,512]{2,1,0:T(8,128)(2,1)} %copy-done.8) | copy-start | bytes 1572868
  458.0 25.7 %copy-start.55 = (f32[2,256]{1,0:T(2,128)S(1)}, f32[2,256]{1,0:T(2,128)}, u32[]{:S(2)}) copy-start(f32[2,256]{1,0:T(2,128)} %copy-done.54) | copy-start | bytes 6148
  458.0 25.7 %copy-start.59 = (f32[512]{0:T(512)S(1)}, f32[512]{0:T(512)}, u32[]{:S(2)}) copy-start(f32[512]{0:T(512)} %copy-done.58) | copy-start | bytes 6148
  460.5 24.6 %copy-start.67 = (f32[2,256]{1,0:T(2,128)S(1)}, f32[2,256]{1,0:T(2,128)}, u32[]{:S(2)}) copy-start(f32[2,256]{1,0:T(2,128)} %copy-done.66) | copy-start | bytes 6148
  460.5 24.7 %copy-start.63 = (f32[2,256]{1,0:T(2,128)S(1)}, f32[2,256]{1,0:T(2,128)}, u32[]{:S(2)}) copy-start(f32[2,256]{1,0:T(2,128)} %copy-done.62) | copy-start | bytes 6148
  460.5 26.5 %copy-start.5 = (bf16[2,256,512]{2,1,0:T(8,128)(2,1)S(1)}, bf16[2,256,512]{2,1,0:T(8,128)(2,1)}, u32[]{:S(2)}) copy-start(bf16[2,256,512]{2,1,0:T(8,128)(2,1)} %copy-done.4) | copy-start | bytes 1572868
  460.5 26.5 %copy-start.14 = (bf16[2,256,512]{2,1,0:T(8,128)(2,1)S(1)}, bf16[2,256,512]{2,1,0:T(8,128)(2,1)}, u32[]{:S(2)}) copy-start(bf16[2,256,512]{2,1,0:T(8,128)(2,1)} %reduce-scatter.9.cloned.1.call-done) | copy-start | bytes 1572868
  460.5 26.5 %copy-start.22 = (bf16[2,256,512]{2,1,0:T(8,128)(2,1)S(1)}, bf16[2,256,512]{2,1,0:T(8,128)(2,1)}, u32[]{:S(2)}) copy-start(bf16[2,256,512]{2,1,0:T(8,128)(2,1)} %param.43) | copy-start | bytes 1572868
  460.5 26.5 %copy-start.53 = (f32[2,256]{1,0:T(2,128)S(1)}, f32[2,256]{1,0:T(2,128)}, u32[]{:S(2)}) copy-start(f32[2,256]{1,0:T(2,128)} %copy-done.52) | copy-start | bytes 6148
  460.5 26.5 %copy-start.57 = (f32[512]{0:T(512)S(1)}, f32[512]{0:T(512)}, u32[]{:S(2)}) copy-start(f32[512]{0:T(512)} %copy-done.56) | copy-start | bytes 6148
  460.5 26.5 %copy-start.61 = (f32[2,256]{1,0:T(2,128)S(1)}, f32[2,256]{1,0:T(2,128)}, u32[]{:S(2)}) copy-start(f32[2,256]{1,0:T(2,128)} %copy-done.60) | copy-start | bytes 6148
  460.5 26.5 %copy-start.65 = (f32[2,256]{1,0:T(2,128)S(1)}, f32[2,256]{1,0:T(2,128)}, u32[]{:S(2)}) copy-start(f32[2,256]{1,0:T(2,128)} %copy-done.64) | copy-start | bytes 6148
  460.5 26.5 %copy-start.69 = (f32[2,256]{1,0:T(2,128)S(1)}, f32[2,256]{1,0:T(2,128)}, u32[]{:S(2)}) copy-start(f32[2,256]{1,0:T(2,128)} %copy-done.68) | copy-start | bytes 6148
  462.0 27.7 %copy-start.29 = (bf16[2,256,1,512]{3,2,1,0:T(2,128)(2,1)S(1)}, bf16[2,256,1,512]{3,2,1,0:T(2,128)(2,1)}, u32[]{:S(2)}) copy-start(bf16[2,256,1,512]{3,2,1,0:T(2,128)(2,1)} %copy-done.28) | copy-start | bytes 1572868
  532.1 15.5 %copy-start.72 = (f32[512]{0:T(512)S(1)}, f32[512]{0:T(512)}, u32[]{:S(2)}) copy-start(f32[512]{0:T(512)} %get-tuple-element.24) | copy-start | bytes 6148
  532.1 15.6 %copy-start.73 = (f32[512]{0:T(512)S(1)}, f32[512]{0:T(512)}, u32[]{:S(2)}) copy-start(f32[512]{0:T(512)} %get-tuple-element.29) | copy-start | bytes 6148
  568.3 26.2 %copy-start.1 = (bf16[512,256]{1,0:T(8,128)(2,1)S(1)}, bf16[512,256]{1,0:T(8,128)(2,1)}, u32[]{:S(2)}) copy-start(bf16[512,256]{1,0:T(8,128)(2,1)} %param.39) | copy-start | bytes 786436
  (42 other events, 228.5 us)
Sparse Core Ops, SparseCore 0:
  48.7 31.2 all-gather.7
  120.6 31.4 reduce-scatter.4
  155.0 30.8 all-gather.9
  187.4 28.6 all-gather.11
  228.6 31.4 reduce-scatter.8
  262.2 33.7 reduce-scatter.6
  299.8 30.9 all-gather.13
  452.2 31.4 reduce-scatter.10
  526.8 61.8 all-reduce.4
where the time goes:
time: 610 us; the launch traced here: 601 us
  waiting for transfers between devices  238 us (39%)
  matrix products  215 us (35%)
  blocking collectives  64.5 us (11%)
  other arithmetic  40.6 us (7%)
  local copies, waits for them, and re-layouts  25.6 us (4%)
  between operations  15.4 us (3%)
    dot_general x31, matrix products, contract(): return jnp.einsum(pattern, lhs, rhs, preferred_element_type=jnp.float32)  200 us
    reduce_scatter x1, waiting for transfers between devices, device_step(): lax.psum_scatter(contract('btf,fd->btd', fc_hidden, w_fc2).astype(jnp.bfl...  32.3 us
    reduce_scatter x1, waiting for transfers between devices, device_step(): lax.psum_scatter(contract('btc,cd->btd', attn_flat, w_out).astype(jnp.bfl...  31.5 us
    all_gather x1, waiting for transfers between devices, device_step(): norm_one_all = lax.all_gather(norm_one, 'tp', axis=1, tiled=True)  31.1 us
    all_gather x1, waiting for transfers between devices, device_step(): lax.all_gather(d_mid.astype(jnp.bfloat16), 'tp', axis=1, tiled=True)  30.8 us
    all_gather x1, waiting for transfers between devices, device_step(): norm_two_all = lax.all_gather(norm_two, 'tp', axis=1, tiled=True)  29.9 us
    reduce_scatter x1, waiting for transfers between devices, device_step(): lax.psum_scatter(contract('btf,df->btd', d_fc_low, w_fc1).astype(jnp.bflo...  27.3 us
    reduce_scatter x1, waiting for transfers between devices, device_step(): lax.psum_scatter(d_norm_one_part.astype(jnp.bfloat16), 'tp', scatter_dime...  21.6 us
  transfers between devices with their start and end apart: 9, of which 9 were waited for; matrix products, arithmetic and copies ran while one was open for 6% of the time, Pallas kernels for 0%

commit v1 on v0

v1 whole, which is shorter than its diff:
```python
import functools
import math
import jax
import jax.numpy as jnp
from jax import lax
from jax.experimental import pallas as pl
from jax.experimental.pallas import tpu as pltpu
from jax.sharding import PartitionSpec as P

HEAD_DIM = 64
LN_EPS = 1e-5
BF = jnp.bfloat16
F32 = jnp.float32
LANES = 128
BIAS_ROWS = 16
VEC_ROWS = 8


def dims(lhs, rhs, contract_lhs, contract_rhs):
    return lax.dot_general(lhs, rhs, (((contract_lhs,), (contract_rhs,)), ((), ())), preferred_element_type=F32)


def mm(lhs, rhs):
    return dims(lhs, rhs, 1, 0)


def mm_nt(lhs, rhs):
    return dims(lhs, rhs, 1, 1)


def mm_tn(lhs, rhs):
    return dims(lhs, rhs, 0, 0)


def phi_cdf(x):
    return 0.5 * (1.0 + lax.erf(x * (0.5 ** 0.5)))


def gelu(x):
    return x * phi_cdf(x)


def gelu_grad(x):
    return phi_cdf(x) + x * (jnp.exp(x * x * -0.5) * (1.0 / math.sqrt(2.0 * math.pi)))


def norm_stats(x):
    centred = x - jnp.mean(x, axis=-1, keepdims=True)
    rstd = lax.rsqrt(jnp.mean(centred * centred, axis=-1, keepdims=True) + LN_EPS)
    return centred * rstd, rstd


def norm_back(d_out, x_hat, rstd, gain):
    a = d_out * gain
    return rstd * (a - jnp.mean(a, axis=-1, keepdims=True) - x_hat * jnp.mean(a * x_hat, axis=-1, keepdims=True))


def colsum(x):
    return jnp.sum(x, axis=0, keepdims=True)


def peer(index):
    return {'tp': index}


def entry_barrier(size, me):
    barrier = pltpu.get_barrier_semaphore()
    for step in range(1, size):
        pl.semaphore_signal(barrier, inc=1, device_id=peer(lax.rem(me + step, size)), device_id_type=pl.DeviceIdType.MESH)
    pl.semaphore_wait(barrier, size - 1)


def exchange_kernel(size, x_ref, out_ref, send_sem, recv_sem, own_sem):
    me = lax.axis_index('tp')
    entry_barrier(size, me)
    copies = []
    for step in range(1, size):
        to = lax.rem(me + step, size)
        copies.append(pltpu.make_async_remote_copy(
            src_ref=x_ref.at[to], dst_ref=out_ref.at[me], send_sem=send_sem.at[step], recv_sem=recv_sem.at[step],
            device_id=peer(to), device_id_type=pl.DeviceIdType.MESH))
        copies[-1].start()
    own = pltpu.make_async_copy(x_ref.at[me], out_ref.at[me], own_sem)
    own.start()
    own.wait()
    for copy in copies:
        copy.wait()


def exchange(x, size, cid):
    return pl.pallas_call(
        functools.partial(exchange_kernel, size),
        out_shape=jax.ShapeDtypeStruct(x.shape, x.dtype),
        in_specs=[pl.BlockSpec(memory_space=pltpu.VMEM)],
        out_specs=pl.BlockSpec(memory_space=pl.ANY),
        scratch_shapes=[pltpu.SemaphoreType.DMA((size,)), pltpu.SemaphoreType.DMA((size,)), pltpu.SemaphoreType.DMA],
        compiler_params=pltpu.CompilerParams(collective_id=cid, has_side_effects=True),
        name=f'exchange{cid}',
    )(x)


def all_sum_kernel(size, x_ref, out_ref, parts, mine, whole, send_a, recv_a, send_b, recv_b):
    me = lax.axis_index('tp')
    entry_barrier(size, me)
    copies = []
    for step in range(1, size):
        to = lax.rem(me + step, size)
        copies.append(pltpu.make_async_remote_copy(
            src_ref=x_ref.at[to], dst_ref=parts.at[step], send_sem=send_a.at[step], recv_sem=recv_a.at[step],
            device_id=peer(to), device_id_type=pl.DeviceIdType.MESH))
        copies[-1].start()
    for copy in copies:
        copy.wait()
    total = x_ref[me].astype(F32)
    for step in range(1, size):
        total = total + parts[step].astype(F32)
    mine[...] = total.astype(BF)
    copies = []
    for step in range(1, size):
        to = lax.rem(me + step, size)
        copies.append(pltpu.make_async_remote_copy(
            src_ref=mine, dst_ref=whole.at[me], send_sem=send_b.at[step], recv_sem=recv_b.at[step],
            device_id=peer(to), device_id_type=pl.DeviceIdType.MESH))
        copies[-1].start()
    for copy in copies:
        copy.wait()
    out_ref[...] = whole[...].astype(F32)
    out_ref[me] = mine[...].astype(F32)


def all_sum(x, size, cid):
    return pl.pallas_call(
        functools.partial(all_sum_kernel, size),
        out_shape=jax.ShapeDtypeStruct(x.shape, F32),
        in_specs=[pl.BlockSpec(memory_space=pltpu.VMEM)],
        out_specs=pl.BlockSpec(memory_space=pltpu.VMEM),
        scratch_shapes=[pltpu.VMEM(x.shape, BF), pltpu.VMEM(x.shape[1:], BF), pltpu.VMEM(x.shape, BF)]
        + [pltpu.SemaphoreType.DMA((size,))] * 4,
        compiler_params=pltpu.CompilerParams(collective_id=cid, has_side_effects=True),
        name=f'all_sum{cid}',
    )(x)


def load_mel(m_scr, mel_ref, halo_ref):
    mel_len, n_mel = mel_ref.shape[1:]
    total = m_scr.shape[0]
    m_scr[0:8, :] = jnp.zeros((8, m_scr.shape[1]), F32)
    m_scr[8 + mel_len:total, :] = jnp.zeros((total - 8 - mel_len, m_scr.shape[1]), F32)
    m_scr[8:8 + mel_len, 0:n_mel] = mel_ref[0].astype(F32)
    halo = halo_ref[0].astype(F32)
    m_scr[6:8, 0:n_mel] = halo[0:2]
    m_scr[8 + mel_len:10 + mel_len, 0:n_mel] = halo[2:4]


def mel_taps(m_scr, rows, n_mel):
    return [m_scr[pl.ds(5 + tap, rows, stride=2), :].astype(BF)[:, 0:n_mel] for tap in range(4)]


def conv_one(taps, w_ref, bias):
    even = mm(taps[0], w_ref[0]) + mm(taps[1], w_ref[1]) + mm(taps[2], w_ref[2]) + bias
    odd = mm(taps[1], w_ref[0]) + mm(taps[2], w_ref[1]) + mm(taps[3], w_ref[2]) + bias
    return even, odd


def row_ids(rows, width):
    return lax.broadcasted_iota(jnp.int32, (rows, width), 0)


def front_kernel(mel_ref, halo_ref, pos_ref, w1_ref, w2_ref, vec_ref, h1_ref, h2_ref, x_ref, n1_ref, m_scr, e_scr, o_scr):
    rank = lax.axis_index('tp')
    n_mel = mel_ref.shape[2]
    frames, width = pos_ref.shape
    rows = e_scr.shape[0]
    load_mel(m_scr, mel_ref, halo_ref)
    even, odd = conv_one(mel_taps(m_scr, rows, n_mel), w1_ref, vec_ref[0:1, :])
    e_scr[...] = gelu(even)
    o_scr[...] = gelu(odd)

    @pl.when(rank == 0)
    def _():
        o_scr[0:1, :] = jnp.zeros((1, width), F32)

    h1_ref[0, :, 0:width] = o_scr[0:frames, :].astype(BF)
    h1_ref[0, :, width:2 * width] = e_scr[1:frames + 1, :].astype(BF)
    h1_ref[0, :, 2 * width:3 * width] = o_scr[1:frames + 1, :].astype(BF)
    h2_pre = mm(h1_ref[0], w2_ref[...]) + vec_ref[1:2, :]
    h2_ref[0] = h2_pre
    x_low = (gelu(h2_pre) + pos_ref[...]).astype(BF)
    x_ref[0] = x_low
    x_hat, _ = norm_stats(x_low.astype(F32))
    n1_ref[0] = (x_hat * vec_ref[2:3, :] + vec_ref[3:4, :]).astype(BF)


def front(mel, halo, pos, w1, w2, vec):
    n_batch, mel_len, n_mel = mel.shape
    frames, width = pos.shape
    rows = frames + 8
    per = lambda *shape: pl.BlockSpec((1,) + shape, lambda b: (b,) + (0,) * len(shape))
    whole = lambda a: pl.BlockSpec(a.shape, lambda b: (0,) * a.ndim)
    return pl.pallas_call(
        front_kernel, grid=(n_batch,),
        in_specs=[per(mel_len, n_mel), per(4, n_mel), whole(pos), whole(w1), whole(w2), whole(vec)],
        out_specs=[per(frames, 3 * width), per(frames, width), per(frames, width), per(frames, width)],
        out_shape=[jax.ShapeDtypeStruct((n_batch, frames, 3 * width), BF), jax.ShapeDtypeStruct((n_batch, frames, width), F32),
                   jax.ShapeDtypeStruct((n_batch, frames, width), BF), jax.ShapeDtypeStruct((n_batch, frames, width), BF)],
        scratch_shapes=[pltpu.VMEM((2 * rows + 8, LANES), F32), pltpu.VMEM((rows, width), F32), pltpu.VMEM((rows, width), F32)],
        cost_estimate=pl.CostEstimate(flops=8_000_000_000, bytes_accessed=8_000_000, transcendentals=0),
        name='front',
    )(mel, halo, pos, w1, w2, vec)


def project_kernel(g_ref, n1_ref, out_ref):
    heads, n_batch, rows3, frames = out_ref.shape
    width = n1_ref.shape[2]
    w_all = g_ref[:, 0:rows3, 0:width].reshape(heads * rows3, width)
    bias = g_ref[:, 0:rows3, width:width + 1].astype(F32).reshape(heads * rows3, 1)
    for b in range(n_batch):
        out_ref[:, b] = (mm_nt(w_all, n1_ref[b]) + bias).astype(BF).reshape(heads, rows3, frames)


def project(g, n1, rows3):
    heads = g.shape[0]
    n_batch, frames, _ = n1.shape
    return pl.pallas_call(
        project_kernel, out_shape=jax.ShapeDtypeStruct((heads, n_batch, rows3, frames), BF),
        in_specs=[pl.BlockSpec(memory_space=pltpu.VMEM)] * 2, out_specs=pl.BlockSpec(memory_space=pltpu.VMEM),
        cost_estimate=pl.CostEstimate(flops=2_000_000_000, bytes_accessed=4_000_000, transcendentals=0),
        name='project',
    )(g, n1)


def attend_kernel(qkv_ref, o_ref, p_ref, k_scr, v_scr, s_scr0, s_scr1):
    step = pl.program_id(1)
    parts, _, _, frames = qkv_ref.shape
    hd = HEAD_DIM

    @pl.when(step == 0)
    def _():
        for part in range(parts):
            k_scr[part * frames:(part + 1) * frames, :] = qkv_ref[part, 0, hd:2 * hd, :].astype(F32).T.astype(BF)
            v_scr[:, part * frames:(part + 1) * frames] = qkv_ref[part, 0, 2 * hd:3 * hd, :]

    factor = HEAD_DIM ** -0.5 * math.log2(math.e)
    scrs = (s_scr0, s_scr1)
    tops = []
    for sub in range(2):
        q_t = qkv_ref[step * 2 + sub, 0, 0:hd, :]
        top = None
        for part in range(parts):
            rows = slice(part * frames, (part + 1) * frames)
            s = mm(k_scr[rows, :], q_t)
            scrs[sub][rows, :] = s
            part_top = jnp.max(s.reshape(frames // 8, 8, frames), axis=0)
            top = part_top if top is None else jnp.maximum(top, part_top)
        tops.append(jnp.max(top, axis=0, keepdims=True))
    invs = []
    for sub in range(2):
        total = jnp.zeros((8, frames), F32)
        for part in range(parts):
            rows = slice(part * frames, (part + 1) * frames)
            e = jnp.exp2((scrs[sub][rows, :] - tops[sub]) * factor)
            scrs[sub][rows, :] = e
            total = total + jnp.sum(e.reshape(frames // 8, 8, frames), axis=0)
        invs.append(1.0 / jnp.sum(total, axis=0, keepdims=True))
    for sub in range(2):
        out = jnp.zeros((hd, frames), F32)
        for part in range(parts):
            rows = slice(part * frames, (part + 1) * frames)
            p = (scrs[sub][rows, :] * invs[sub]).astype(BF)
            p_ref[0, sub, rows, :] = p
            out = out + mm(v_scr[:, rows], p)
        o_ref[sub, 0] = out.astype(BF)


def attend(qkv):
    parts, n_batch, rows3, frames = qkv.shape
    total = parts * frames
    return pl.pallas_call(
        attend_kernel, grid=(n_batch, parts // 2),
        in_specs=[pl.BlockSpec((parts, 1, rows3, frames), lambda b, i: (0, b, 0, 0))],
        out_specs=[pl.BlockSpec((2, 1, HEAD_DIM, frames), lambda b, i: (i, b, 0, 0)),
                   pl.BlockSpec((1, 2, total, frames), lambda b, i: (b, i, 0, 0))],
        out_shape=[jax.ShapeDtypeStruct((parts, n_batch, HEAD_DIM, frames), BF),
                   jax.ShapeDtypeStruct((n_batch, parts, total, frames), BF)],
        scratch_shapes=[pltpu.VMEM((total, HEAD_DIM), BF), pltpu.VMEM((HEAD_DIM, total), BF),
                        pltpu.VMEM((total, frames), F32), pltpu.VMEM((total, frames), F32)],
        compiler_params=pltpu.CompilerParams(dimension_semantics=('arbitrary', 'arbitrary')),
        cost_estimate=pl.CostEstimate(flops=20_000_000_000, bytes_accessed=20_000_000, transcendentals=0),
        name='attend',
    )(qkv)


def attend_back_kernel(qkv_ref, do_ref, o_ref, p_ref, out_ref, dbias_ref, v_scr, kt_scr, dk_scr, dv_scr, dq_sum):
    b, step = pl.program_id(0), pl.program_id(1)
    parts, _, _, frames = qkv_ref.shape
    hd = HEAD_DIM

    @pl.when(step == 0)
    def _():
        for part in range(parts):
            rows = slice(part * frames, (part + 1) * frames)
            v_scr[rows, :] = qkv_ref[part, 0, 2 * hd:3 * hd, :].astype(F32).T.astype(BF)
            kt_scr[:, rows] = qkv_ref[part, 0, hd:2 * hd, :]
        dk_scr[...] = jnp.zeros_like(dk_scr)
        dv_scr[...] = jnp.zeros_like(dv_scr)

    @pl.when((step == 0) & (b == 0))
    def _():
        dq_sum[...] = jnp.zeros_like(dq_sum)
        dbias_ref[...] = jnp.zeros_like(dbias_ref)

    do_t = do_ref[step, 0]
    q = qkv_ref[step, 0, 0:hd, :].astype(F32).T.astype(BF)
    do = do_t.astype(F32).T.astype(BF)
    delta = colsum(do_t.astype(F32) * o_ref[step, 0].astype(F32))
    dq = jnp.zeros((hd, frames), F32)
    for part in range(parts):
        rows = slice(part * frames, (part + 1) * frames)
        p = p_ref[0, 0, rows, :]
        dp = mm(v_scr[rows, :], do_t)
        ds = (p.astype(F32) * (dp - delta)).astype(BF)
        dv_scr[rows, :] += mm(p, do)
        dk_scr[rows, :] += mm(ds, q)
        dq = dq + mm(kt_scr[:, rows], ds)
    dq = dq * (HEAD_DIM ** -0.5)
    out_ref[step, 0, 0:hd, :] = dq.astype(BF)
    dq_sum[...] += dq

    @pl.when(step == parts - 1)
    def _():
        for part in range(parts):
            rows = slice(part * frames, (part + 1) * frames)
            out_ref[part, 0, hd:2 * hd, :] = (dk_scr[rows, :] * (HEAD_DIM ** -0.5)).T.astype(BF)
            out_ref[part, 0, 2 * hd:3 * hd, :] = dv_scr[rows, :].T.astype(BF)
        dbias_ref[1:2, :] += colsum(dv_scr[...])
        dbias_ref[0:1, :] = colsum(dq_sum[...].T)


def attend_back(qkv, do, o, p):
    parts, n_batch, rows3, frames = qkv.shape
    total = parts * frames
    block = lambda rows: pl.BlockSpec((parts, 1, rows, frames), lambda b, i: (0, b, 0, 0))
    return pl.pallas_call(
        attend_back_kernel, grid=(n_batch, parts),
        in_specs=[block(rows3), block(HEAD_DIM), block(HEAD_DIM), pl.BlockSpec((1, 1, total, frames), lambda b, i: (b, i, 0, 0))],
        out_specs=[block(rows3), pl.BlockSpec((8, HEAD_DIM), lambda b, i: (0, 0))],
        out_shape=[jax.ShapeDtypeStruct(qkv.shape, BF), jax.ShapeDtypeStruct((8, HEAD_DIM), F32)],
        scratch_shapes=[pltpu.VMEM((total, HEAD_DIM), BF), pltpu.VMEM((HEAD_DIM, total), BF),
                        pltpu.VMEM((total, HEAD_DIM), F32), pltpu.VMEM((total, HEAD_DIM), F32), pltpu.VMEM((HEAD_DIM, frames), F32)],
        compiler_params=pltpu.CompilerParams(dimension_semantics=('arbitrary', 'arbitrary')),
        cost_estimate=pl.CostEstimate(flops=40_000_000_000, bytes_accessed=20_000_000, transcendentals=0),
        name='attend_back',
    )(qkv, do, o, p)


def mlp_kernel(o_ref, x_ref, dy_ref, wo_ref, w1_ref, w2_ref, vec_ref, y_ref, da_ref, dmid_ref, dwo_ref, dw1_ref, dw2_ref, dvec_ref,
               mid_scr, n2_scr, y_scr, dn_scr, hat_scr, rstd_scr):
    j = pl.program_id(0)
    heads, n_batch, hd, frames = o_ref.shape
    rows, width = x_ref.shape
    fc = w2_ref.shape[1]

    @pl.when(j == 0)
    def _():
        wo = wo_ref[:, :, 0:width].reshape(heads * hd, width)
        for b in range(n_batch):
            blk = slice(b * frames, (b + 1) * frames)
            attn = mm_tn(o_ref[:, b].reshape(heads * hd, frames), wo)
            mid = (x_ref[blk, :].astype(F32) + attn + vec_ref[4:5, :]).astype(BF)
            mid_scr[blk, :] = mid
            x_hat, rstd = norm_stats(mid.astype(F32))
            hat_scr[blk, :] = x_hat
            rstd_scr[blk, :] = jnp.broadcast_to(rstd, (frames, LANES))
            n2_scr[blk, :] = (x_hat * vec_ref[5:6, :] + vec_ref[6:7, :]).astype(BF)
        y_scr[...] = jnp.zeros_like(y_scr)
        dn_scr[...] = jnp.zeros_like(dn_scr)

    w1 = w1_ref[0, 0:width, :]
    pre = mm(n2_scr[...], w1) + w1_ref[0, width:width + 1, :].astype(F32)
    cdf = phi_cdf(pre)
    hidden = (pre * cdf).astype(BF)
    grad = cdf + pre * (jnp.exp(pre * pre * -0.5) * (1.0 / math.sqrt(2.0 * math.pi)))
    d_pre = mm_nt(dy_ref[...], w2_ref[0]) * grad
    d_low = d_pre.astype(BF)
    y_scr[...] += mm(hidden, w2_ref[0])
    dn_scr[...] += mm_nt(d_low, w1)
    dw2_ref[0] = mm_tn(hidden, dy_ref[...]).astype(BF)
    dw1_ref[0, 0:width, :] = mm_tn(n2_scr[...], d_low).astype(BF)
    dw1_ref[0, width:width + BIAS_ROWS, :] = jnp.broadcast_to(colsum(d_pre), (BIAS_ROWS, fc)).astype(BF)

    @pl.when(j == pl.num_programs(0) - 1)
    def _():
        wo = wo_ref[:, :, 0:width].reshape(heads * hd, width)
        y_ref[...] = (mid_scr[...].astype(F32) + y_scr[...] + vec_ref[7:8, :]).astype(BF)
        dvec_ref[...] = jnp.zeros_like(dvec_ref)
        d_wo = jnp.zeros((heads * hd, width), F32)
        for b in range(n_batch):
            blk = slice(b * frames, (b + 1) * frames)
            dy = dy_ref[blk, :].astype(F32)
            x_hat = hat_scr[blk, :]
            d_n2 = dn_scr[blk, :]
            d_mid = dy + norm_back(d_n2, x_hat, rstd_scr[blk, 0:1], vec_ref[5:6, :])
            dmid_ref[blk, :] = d_mid
            dvec_ref[0:1, :] += colsum(dy)
            dvec_ref[1:2, :] += colsum(d_n2 * x_hat)
            dvec_ref[2:3, :] += colsum(d_n2)
            dvec_ref[3:4, :] += colsum(d_mid)
            mid_low = d_mid.astype(BF)
            da_ref[:, b] = mm_nt(wo, mid_low).astype(BF).reshape(heads, hd, frames)
            d_wo = d_wo + mm(o_ref[:, b].reshape(heads * hd, frames), mid_low)
        dwo_ref[...] = d_wo.astype(BF).reshape(heads, hd, width)


def mlp(o, x, dy, g, w1, w2, vec):
    heads, n_batch, hd, frames = o.shape
    rows, width = x.shape
    chunks, fc, _ = w2.shape
    whole = lambda shape: pl.BlockSpec(shape, lambda j: (0,) * len(shape))
    chunk = lambda shape: pl.BlockSpec((1,) + shape[1:], lambda j: (j,) + (0,) * (len(shape) - 1))
    sds = jax.ShapeDtypeStruct
    outs = [sds((rows, width), BF), sds((heads, n_batch, hd, frames), BF), sds((rows, width), F32), sds((heads, hd, width), BF),
            sds(w1.shape, BF), sds(w2.shape, BF), sds((VEC_ROWS, width), F32)]
    return pl.pallas_call(
        mlp_kernel, grid=(chunks,),
        in_specs=[whole(o.shape), whole(x.shape), whole(dy.shape),
                  pl.BlockSpec((heads, hd, g.shape[2]), lambda j: (0, g.shape[1] // hd - 1, 0)),
                  chunk(w1.shape), chunk(w2.shape), whole(vec.shape)],
        out_specs=[whole(s.shape) for s in outs[:4]] + [chunk(w1.shape), chunk(w2.shape), whole(outs[6].shape)],
        out_shape=outs,
        scratch_shapes=[pltpu.VMEM((rows, width), BF), pltpu.VMEM((rows, width), BF), pltpu.VMEM((rows, width), F32),
                        pltpu.VMEM((rows, width), F32), pltpu.VMEM((rows, width), F32), pltpu.VMEM((rows, LANES), F32)],
        compiler_params=pltpu.CompilerParams(dimension_semantics=('arbitrary',)),
        cost_estimate=pl.CostEstimate(flops=14_000_000_000, bytes_accessed=12_000_000, transcendentals=0),
        name='mlp',
    )(o, x, dy, g, w1, w2, vec)


def embed_back_kernel(dqkv_ref, g_ref, n1_ref, x_ref, dmid_ref, h2_ref, h1_ref, dwo_ref, vec_ref, dh2_ref, dw_ref, dw2_ref, dvec_ref):
    heads, n_batch, rows3, frames = dqkv_ref.shape
    width = n1_ref.shape[2]
    w_all = g_ref[:, 0:rows3, 0:width].reshape(heads * rows3, width)
    dvec_ref[...] = jnp.zeros_like(dvec_ref)
    d_all = [dqkv_ref[:, b].reshape(heads * rows3, frames) for b in range(n_batch)]
    for b in range(n_batch):
        d_n1 = mm_tn(d_all[b], w_all)
        x_hat, rstd = norm_stats(x_ref[b].astype(F32))
        d_x = dmid_ref[b * frames:(b + 1) * frames, :] + norm_back(d_n1, x_hat, rstd, vec_ref[2:3, :])
        d_h2 = d_x * gelu_grad(h2_ref[b])
        dvec_ref[0:1, :] += colsum(d_n1 * x_hat)
        dvec_ref[1:2, :] += colsum(d_n1)
        dvec_ref[2:3, :] += colsum(d_h2)
        dh2_ref[b] = d_h2.astype(BF)
    d_w = mm(d_all[0], n1_ref[0])
    d_conv = mm_tn(h1_ref[0], dh2_ref[0])
    for b in range(1, n_batch):
        d_w = d_w + mm(d_all[b], n1_ref[b])
        d_conv = d_conv + mm_tn(h1_ref[b], dh2_ref[b])
    dw_ref[:, 0:rows3, :] = d_w.astype(BF).reshape(heads, rows3, width)
    dw_ref[:, rows3:, :] = dwo_ref[...]
    dw2_ref[...] = d_conv.astype(BF)


def embed_back(dqkv, g, n1, x, dmid, h2, h1, dwo, vec):
    n_batch, frames, width = n1.shape
    heads = dqkv.shape[0]
    sds = jax.ShapeDtypeStruct
    return pl.pallas_call(
        embed_back_kernel,
        in_specs=[pl.BlockSpec(memory_space=pltpu.VMEM)] * 9,
        out_specs=[pl.BlockSpec(memory_space=pltpu.VMEM)] * 4,
        out_shape=[sds((n_batch, frames, width), BF), sds((heads, g.shape[1], width), BF), sds((3 * width, width), BF),
                   sds((VEC_ROWS, width), F32)],
        cost_estimate=pl.CostEstimate(flops=8_000_000_000, bytes_accessed=8_000_000, transcendentals=0),
        name='embed_back',
    )(dqkv, g, n1, x, dmid, h2, h1, dwo, vec)


def stem_back_kernel(mel_ref, halo_ref, dh2_ref, edge_ref, w1_ref, w2_ref, vec_ref, dmel_ref, dw_ref, db_ref,
                     m_scr, d_scr, e_scr, o_scr, out_scr):
    rank = lax.axis_index('tp')
    first = pl.program_id(0) == 0
    n_mel = mel_ref.shape[2]
    frames, width = dh2_ref.shape[1:]
    rows = e_scr.shape[0]
    load_mel(m_scr, mel_ref, halo_ref)
    taps = mel_taps(m_scr, rows, n_mel)
    even, odd = conv_one(taps, w1_ref, vec_ref[0:1, :])
    d_scr[0:8, :] = jnp.zeros((8, width), F32)
    d_scr[frames:frames + 16, :] = jnp.zeros((16, width), F32)
    d_scr[1:frames + 1, :] = dh2_ref[0].astype(F32)
    edge = edge_ref[0].astype(F32)
    d_scr[0:1, :] = edge[0:1]
    d_scr[frames + 1:frames + 2, :] = edge[1:2]
    here = d_scr[0:rows, :].astype(BF)
    after = d_scr[1:rows + 1, :].astype(BF)
    ids = row_ids(rows, width)
    own = (ids >= 1) & (ids <= frames)
    d_even = jnp.where((ids >= 1) & (ids <= frames + 1), mm_nt(here, w2_ref[width:2 * width, :]) * gelu_grad(even), 0.0)
    lowest = jnp.where(rank == 0, 1, 0)
    d_odd = mm_nt(here, w2_ref[2 * width:3 * width, :]) + mm_nt(after, w2_ref[0:width, :])
    d_odd = jnp.where((ids >= lowest) & (ids <= frames), d_odd * gelu_grad(odd), 0.0)
    e_own = jnp.where(own, d_even, 0.0)
    o_own = jnp.where(own, d_odd, 0.0)
    d_bias = colsum(e_own) + colsum(o_own)
    e_own, o_own = e_own.astype(BF), o_own.astype(BF)
    d_w = [mm_tn(taps[t], e_own) + mm_tn(taps[t + 1], o_own) for t in range(3)]

    @pl.when(first)
    def _():
        db_ref[...] = jnp.zeros_like(db_ref)
        dw_ref[...] = jnp.zeros_like(dw_ref)

    db_ref[0:1, :] += d_bias
    for t in range(3):
        dw_ref[t] += d_w[t]
    e_scr[...] = d_even
    o_scr[...] = d_odd
    e_here = e_scr[1:frames + 1, :].astype(BF)
    e_after = e_scr[2:frames + 2, :].astype(BF)
    o_here = o_scr[1:frames + 1, :].astype(BF)
    o_before = o_scr[0:frames, :].astype(BF)
    out_scr[pl.ds(0, frames, stride=2), 0:n_mel] = (mm_nt(e_here, w1_ref[1]) + mm_nt(o_here, w1_ref[0]) + mm_nt(o_before, w1_ref[2]))
    out_scr[pl.ds(1, frames, stride=2), 0:n_mel] = (mm_nt(e_here, w1_ref[2]) + mm_nt(o_here, w1_ref[1]) + mm_nt(e_after, w1_ref[0]))
    dmel_ref[0] = out_scr[:, 0:n_mel].astype(BF)


def stem_back(mel, halo, dh2, edge, w1, w2, vec):
    n_batch, mel_len, n_mel = mel.shape
    frames, width = dh2.shape[1:]
    rows = frames + 8
    per = lambda *shape: pl.BlockSpec((1,) + shape, lambda b: (b,) + (0,) * len(shape))
    whole = lambda shape: pl.BlockSpec(shape, lambda b: (0,) * len(shape))
    sds = jax.ShapeDtypeStruct
    return pl.pallas_call(
        stem_back_kernel, grid=(n_batch,),
        in_specs=[per(mel_len, n_mel), per(4, n_mel), per(frames, width), per(2, width), whole(w1.shape), whole(w2.shape),
                  whole(vec.shape)],
        out_specs=[per(mel_len, n_mel), whole(w1.shape), whole((VEC_ROWS, width))],
        out_shape=[sds(mel.shape, BF), sds(w1.shape, F32), sds((VEC_ROWS, width), F32)],
        scratch_shapes=[pltpu.VMEM((2 * rows + 8, LANES), F32), pltpu.VMEM((frames + 16, width), F32),
                        pltpu.VMEM((rows, width), F32), pltpu.VMEM((rows, width), F32), pltpu.VMEM((mel_len, LANES), F32)],
        compiler_params=pltpu.CompilerParams(dimension_semantics=('arbitrary',)),
        cost_estimate=pl.CostEstimate(flops=8_000_000_000, bytes_accessed=8_000_000, transcendentals=0),
        name='stem_back',
    )(mel, halo, dh2, edge, w1, w2, vec)


def device_step(mel_in, pos_table, w_conv1, b_conv1, w_conv2, b_conv2, ln1_gain, ln1_bias, w_query, b_query,
                w_key, w_value, b_value, w_out, b_out, ln2_gain, ln2_bias, w_fc1, b_fc1, w_fc2, b_fc2, grad_y,
                group_size):
    n_batch, mel_len, n_mel = mel_in.shape
    frames, width = pos_table.shape
    fc = w_fc1.shape[1]
    hd = w_query.shape[1]
    rows3 = 3 * hd
    rows = n_batch * frames
    to_right = [(i, i + 1) for i in range(group_size - 1)]
    to_left = [(i + 1, i) for i in range(group_size - 1)]

    left = lax.ppermute(mel_in[:, -2:], 'tp', to_right)
    right = lax.ppermute(mel_in[:, :2], 'tp', to_left)
    halo = jnp.concatenate([left, right], axis=1)
    vec = jnp.stack([b_conv1, b_conv2, ln1_gain, ln1_bias, b_out, ln2_gain, ln2_bias, b_fc2]).astype(F32)
    w2_flat = w_conv2.reshape(3 * width, width)

    heads_w = jnp.concatenate([jnp.concatenate([w_query, w_key, w_value], axis=1).T, w_out], axis=0)
    heads_b = jnp.concatenate([b_query, jnp.zeros_like(b_query), b_value, jnp.zeros_like(b_query)])
    gathered = lax.all_gather(jnp.concatenate([heads_w, jnp.broadcast_to(heads_b[:, None], (4 * hd, LANES))], axis=1), 'tp')
    fc1_all = lax.all_gather(jnp.concatenate([w_fc1, jnp.broadcast_to(b_fc1[None], (BIAS_ROWS, fc))], axis=0), 'tp')
    fc2_all = lax.all_gather(w_fc2, 'tp')

    h1, h2_pre, x_embed, norm_one = front(mel_in, halo, pos_table, w_conv1, w2_flat, vec)
    qkv = exchange(project(gathered, norm_one, rows3), group_size, 0)
    o_heads, probs = attend(qkv)
    o_all = exchange(o_heads, group_size, 1)
    y_out, d_attn, d_mid, d_wo, d_fc1, d_fc2, vec_mlp = mlp(
        o_all, x_embed.reshape(rows, width), grad_y.reshape(rows, width), gathered, fc1_all, fc2_all, vec)
    fc1_own = lax.psum_scatter(d_fc1, 'tp', scatter_dimension=0).astype(F32)
    fc2_own = lax.psum_scatter(d_fc2, 'tp', scatter_dimension=0).astype(F32)
    d_o = exchange(d_attn, group_size, 2)
    d_heads, d_bias = attend_back(qkv, d_o, o_heads, probs)
    d_qkv = exchange(d_heads, group_size, 3)
    d_h2, d_w, d_conv2, vec_embed = embed_back(d_qkv, gathered, norm_one, x_embed, d_mid, h2_pre, h1, d_wo, vec)
    edge = jnp.stack([lax.ppermute(d_h2[:, -1], 'tp', to_right), lax.ppermute(d_h2[:, 0], 'tp', to_left)], axis=1)
    heads_own = lax.psum_scatter(d_w, 'tp', scatter_dimension=0).astype(F32)
    conv2_part = lax.psum_scatter(d_conv2.reshape(group_size, -1, width), 'tp', scatter_dimension=0)
    d_conv2_all = lax.all_gather(conv2_part, 'tp').astype(F32).reshape(w_conv2.shape)
    d_mel, d_conv1, vec_stem = stem_back(mel_in, halo, d_h2, edge, w_conv1, w2_flat, vec)
    small = jnp.concatenate([d_conv1.reshape(3 * n_mel, width), vec_mlp[0:4], vec_embed[0:3], vec_stem[0:1],
                             jnp.zeros((8, width), F32)]).astype(BF)
    small = all_sum(small.reshape(group_size, -1, width), group_size, 4).reshape(-1, width)
    d_conv1_all = small[:3 * n_mel].reshape(w_conv1.shape)
    vecs = small[3 * n_mel:]
    return (y_out.reshape(grad_y.shape), d_mel, d_conv1_all, vecs[7], d_conv2_all, vecs[6], vecs[4], vecs[5],
            heads_own[0:hd].T, d_bias[0], heads_own[hd:2 * hd].T, heads_own[2 * hd:3 * hd].T, d_bias[1],
            heads_own[3 * hd:], vecs[3], vecs[1], vecs[2], fc1_own[:width], fc1_own[width], fc2_own, vecs[0])


def solution(mesh):
    group_size = mesh.shape['tp']
    in_specs = (P('dp', 'tp', None), P('tp', None), P(), P(), P(), P(), P(), P(),
                P(None, 'tp'), P('tp'), P(None, 'tp'), P(None, 'tp'), P('tp'), P('tp', None), P(), P(), P(),
                P(None, 'tp'), P('tp'), P('tp', None), P(), P('dp', 'tp', None))
    out_specs = (P('dp', 'tp', None), P('dp', 'tp', None), P('dp', None, None), P('dp'), P('dp', None, None),
                 P('dp'), P('dp'), P('dp'), P('dp', 'tp'), P(('dp', 'tp')), P('dp', 'tp'), P('dp', 'tp'),
                 P(('dp', 'tp')), P(('dp', 'tp'), None), P('dp'), P('dp'), P('dp'), P('dp', 'tp'),
                 P(('dp', 'tp')), P(('dp', 'tp'), None), P('dp'))
    local_step = functools.partial(device_step, group_size=group_size)
    return jax.shard_map(local_step, mesh=mesh, in_specs=in_specs, out_specs=out_specs, check_vma=False)
```

time: 610 us -> 354 us (0.58); the launches traced: 601 us -> 353 us
  matrix products: 215 us -> 0 us
  Pallas kernels: 0 us -> 181 us
  waiting for transfers between devices: 238 us -> 114 us
  blocking collectives: 64.5 us -> 0 us
  other arithmetic: 40.6 us -> 15.2 us
  starting transfers between devices: 1.58 us -> 13.9 us
  local copies, waits for them, and re-layouts: 25.6 us -> 14.3 us
    dot_general x31 -> x0, matrix products: 200 us -> none  [contract(): return jnp.einsum(pattern, lhs, rhs, preferred_element_type=jnp.float32)]
    pallas_call x0 -> x12, Pallas kernels: none -> 181 us  [the longest x4 78.4 us: exchange(): pl.pallas_call(functools.partial(exchange_kernel, size), out_shape=jax.Sh...]
    all_gather x4, waiting for transfers between devices: 105 us -> 30.2 us  [the longest x1 22 us: device_step(): lax.all_gather(conv2_part, 'tp').astype(F32).reshape(w_conv2.shape)]
    all_gather x3 -> x0, blocking collectives: 44 us -> none  [the longest x1 16.3 us: device_step(): tap_edges = lax.all_gather(d_taps[:, 0, 0], 'tp')]
    reduce_scatter x4, waiting for transfers between devices: 113 us -> 78.7 us  [the longest x1 30.9 us: device_step(): fc1_own = lax.psum_scatter(d_fc1, 'tp', scatter_dimension=0).astype(F32)]
    psum x1 -> x0, blocking collectives: 20.5 us -> none  [device_step(): lax.psum((d_w_conv1, d_b_conv1, d_w_conv2, d_b_conv2, d_ln1_gain, d_ln1_b...]
    psum x1 -> x0, waiting for transfers between devices: 19.6 us -> none  [device_step(): lax.psum((d_w_conv1, d_b_conv1, d_w_conv2, d_b_conv2, d_ln1_gain, d_ln1_b...]
    reduce_sum x10 -> x0, other arithmetic: 18.9 us -> none  [the longest x4 8.76 us: norm_f32(): return centred * lax.rsqrt(row_var + LN_EPS) * gain_vec + shift_vec]
  transfers between devices with their start and end apart: 9 -> 12, of which waited for: 9 -> 6; matrix products, arithmetic and copies ran while one was open for 6% -> 6% of each run, Pallas kernels for 0% -> 27%
where the time goes in v1:
time: 354 us; the launch traced here: 353 us
  Pallas kernels  181 us (51%)
  waiting for transfers between devices  114 us (32%)
  other arithmetic  15.2 us (4%)
  between operations  14.6 us (4%)
  local copies, waits for them, and re-layouts  14.3 us (4%)
  starting transfers between devices  13.9 us (4%)
    pallas_call x4, Pallas kernels, exchange(): pl.pallas_call(functools.partial(exchange_kernel, size), out_shape=jax.Sh...  78.4 us
    reduce_scatter x1, waiting for transfers between devices, device_step(): fc1_own = lax.psum_scatter(d_fc1, 'tp', scatter_dimension=0).astype(F32)  30.9 us
    pallas_call x1, Pallas kernels, attend_back(): pl.pallas_call(attend_back_kernel, grid=(n_batch, parts), in_specs=[block...  27.4 us
    reduce_scatter x1, waiting for transfers between devices, device_step(): lax.psum_scatter(d_conv2.reshape(group_size, -1, width), 'tp', scatter_di...  24.7 us
    reduce_scatter x1, waiting for transfers between devices, device_step(): fc2_own = lax.psum_scatter(d_fc2, 'tp', scatter_dimension=0).astype(F32)  23.2 us
    all_gather x1, waiting for transfers between devices, device_step(): lax.all_gather(conv2_part, 'tp').astype(F32).reshape(w_conv2.shape)  22 us
    pallas_call x1, Pallas kernels, attend(): pl.pallas_call(attend_kernel, grid=(n_batch, parts // 2), in_specs=[pl.Bl...  18.4 us
    pallas_call x1, Pallas kernels, all_sum(): pl.pallas_call(functools.partial(all_sum_kernel, size), out_shape=jax.Sha...  15.7 us
  transfers between devices with their start and end apart: 12, of which 6 were waited for; matrix products, arithmetic and copies ran while one was open for 6% of the time, Pallas kernels for 27%

profile of v1, /device:TPU:81, one launch (start us, length us, event | category | flops | bytes accessed | tf_op | source)
XLA Modules:
  0.0 352.9 jit_solution(6430762545138805844)
XLA Ops:
  7.4 1.0 maximum_bitcast_fusion
  8.3 0.8 pad_maximum_fusion.4
  9.2 1.6 pad_maximum_fusion
  10.9 0.7 all-gather.14.cloned.1.call-update
  11.7 0.7 broadcast_in_dim.7
  12.4 1.7 pad_maximum_fusion.1
  14.4 4.6 %collective-permute-start = (bf16[2,2,80]{2,1,0:T(2,128)(2,1)S(1)}, bf16[2,2,80]{2,1,0:T(2,128)(2,1)S(1)}, u32[]{:S(2)}, u32[]{:S(2)}) collective-permute-start(bf16[2,2,80]{2,1,0:T(2,128)(2,1)S(1)} %get-tuple-element.163), channel_id=1, source_target_pairs={{0,1},{1,2},{2,3},{3,4},{4,5},{5,6},{6,7},{8,9},{9,10},{10,11},{11... | collective-permute-start | bytes 1928 | tf_op jit(solution)/shard_map/ppermute | solution.py:560
  19.0 2.0 collective-permute-start.1
  21.2 0.6 convert_element_type.23.vec_ref
  21.8 2.1 collective-permute-done.1
  24.5 5.8 %front.1 = (bf16[2,256,1536]{2,1,0:T(8,128)(2,1)}, f32[2,256,512]{2,1,0:T(8,128)}, bf16[2,256,512]{2,1,0:T(8,128)(2,1)}, bf16[2,256,512]{2,1,0:T(8,128)(2,1)}) custom-call(bf16[2,512,80]{2,1,0:T(8,128)(2,1)} %copy-done, bf16[2,4,80]{2,1,0:T(4,128)(2,1)} %pad_maximum_fusion.3.halo_ref, f32[256,512]{1,0:T(8,128)} %pos_ref.1, bf16[3,80,512]{2,1,0:T(8,128)(2,1)} %w1_ref.3, ...), custom_call_target="tpu_custom_call" | custom-call | flops 8000000000 | bytes 8000000 | tf_op jit(solution)/shard_map/front/pallas_call | solution.py:200
  30.4 8.2 %all-gather.10.cloned.1.call-done = bf16[2048,640]{1,0:T(8,128)(2,1)} async-done(((bf16[256,640]{1,0:T(8,128)(2,1)}), bf16[2048,640]{1,0:T(8,128)(2,1)}) %all-gather.10.cloned.1.call-update) | async-done | bytes 2621456 | tf_op jit(solution)/shard_map/all_gather | solution.py:568
  38.5 4.0 %project.1.x_ref = bf16[8,2,192,256]{3,2,1,0:T(8,128)(2,1)} custom-call(bf16[8,256,640]{2,1,0:T(8,128)(2,1)} %bitcast.76, bf16[2,256,512]{2,1,0:T(8,128)(2,1)} %get-tuple-element.43.n1_ref), custom_call_target="tpu_custom_call" | custom-call | flops 2000000000 | bytes 4000000 | tf_op jit(solution)/shard_map/project/pallas_call | solution.py:224
  42.5 31.2 %exchange0.1.qkv_ref = bf16[8,2,192,256]{3,2,1,0:T(8,128)(2,1)} custom-call(bf16[8,2,192,256]{3,2,1,0:T(8,128)(2,1)} %project.1.x_ref), custom_call_target="tpu_custom_call" | custom-call | tf_op jit(solution)/shard_map/exchange0/pallas_call | solution.py:91
  73.7 18.4 %attend.1 = (bf16[8,2,64,256]{3,2,1,0:T(8,128)(2,1)}, bf16[2,8,2048,256]{3,2,1,0:T(8,128)(2,1)}) custom-call(bf16[8,2,192,256]{3,2,1,0:T(8,128)(2,1)} %exchange0.1.qkv_ref), custom_call_target="tpu_custom_call" | custom-call | flops 20000000000 | bytes 20000000 | tf_op jit(solution)/shard_map/attend/pallas_call | solution.py:278
  92.1 12.2 %exchange1.1.o_ref = bf16[8,2,64,256]{3,2,1,0:T(8,128)(2,1)} custom-call(bf16[8,2,64,256]{3,2,1,0:T(8,128)(2,1)} %get-tuple-element.44.x_ref.o_ref), custom_call_target="tpu_custom_call" | custom-call | tf_op jit(solution)/shard_map/exchange1/pallas_call | solution.py:91
  104.3 15.4 %mlp.1 = (bf16[512,512]{1,0:T(8,128)(2,1)}, bf16[8,2,64,256]{3,2,1,0:T(8,128)(2,1)}, f32[512,512]{1,0:T(8,128)}, bf16[8,64,512]{2,1,0:T(8,128)(2,1)}, bf16[8,528...) custom-call(bf16[8,2,64,256]{3,2,1,0:T(8,128)(2,1)} %exchange1.1.o_ref, ...), custom_call_target="tpu_custom_call" | custom-call | flops 14000000000 | bytes 12000000 | tf_op jit(solution)/shard_map/mlp/pallas_call | solution.py:423
  119.7 12.5 %exchange2.1.do_ref = bf16[8,2,64,256]{3,2,1,0:T(8,128)(2,1)} custom-call(bf16[8,2,64,256]{3,2,1,0:T(8,128)(2,1)} %get-tuple-element.47.x_ref), custom_call_target="tpu_custom_call" | custom-call | tf_op jit(solution)/shard_map/exchange2/pallas_call | solution.py:91
  132.2 27.4 %attend_back.1 = (bf16[8,2,192,256]{3,2,1,0:T(8,128)(2,1)}, f32[8,64]{1,0:T(8,128)}) custom-call(bf16[8,2,192,256]{3,2,1,0:T(8,128)(2,1)} %exchange0.1.qkv_ref, bf16[8,2,64,256]{3,2,1,0:T(8,128)(2,1)} %exchange2.1.do_ref, bf16[8,2,64,256]{3,2,1,0:T(8,128)(2,1)} %get-tuple-element.44.x_ref.o_ref, bf16[2,8,2048,256]{3,2,1,0:T(8,128)(2,1)} %get-tuple-element.48.p_ref), custom_call_target="tpu_custom_call" | custom-call | flops 40000000000 | bytes 20000000 | tf_op jit(solution)/shard_map/attend_back/pallas_call | solution.py:343
  159.6 22.6 %exchange3.1.dqkv_ref = bf16[8,2,192,256]{3,2,1,0:T(8,128)(2,1)} custom-call(bf16[8,2,192,256]{3,2,1,0:T(8,128)(2,1)} %get-tuple-element.49.x_ref), custom_call_target="tpu_custom_call" | custom-call | tf_op jit(solution)/shard_map/exchange3/pallas_call | solution.py:91
  182.1 8.9 %embed_back.1 = (bf16[2,256,512]{2,1,0:T(8,128)(2,1)}, bf16[8,256,512]{2,1,0:T(8,128)(2,1)}, bf16[1536,512]{1,0:T(8,128)(2,1)}, f32[8,512]{1,0:T(8,128)}) custom-call(bf16[8,2,192,256]{3,2,1,0:T(8,128)(2,1)} %exchange3.1.dqkv_ref, bf16[8,256,640]{2,1,0:T(8,128)(2,1)} %bitcast.78, bf16[2,256,512]{2,1,0:T(8,128)(2,1)} %get-tuple-element.43.n1_ref, ...), custom_call_target="tpu_custom_call" | custom-call | flops 8000000000 | bytes 8000000 | tf_op jit(solution)/shard_map/embed_back/pallas_call | solution.py:467
  192.4 0.7 reduce-scatter.9.cloned.1.call-update
  193.2 24.7 %reduce-scatter.5.cloned.1.call-done = bf16[1,192,512]{2,1,0:T(8,128)(2,1)} async-done(((bf16[8,192,512]{2,1,0:T(8,128)(2,1)}), bf16[1,192,512]{2,1,0:T(8,128)(2,1)}) %reduce-scatter.5.cloned.1.call-update) | async-done | bytes 196624 | tf_op jit(solution)/shard_map/reduce_scatter | solution.py:586
  218.0 0.7 fusion.1
  218.7 3.5 %collective-permute-start.2 = (bf16[2,512]{1,0:T(2,128)(2,1)S(1)}, bf16[2,512]{1,0:T(2,128)(2,1)S(1)}, u32[]{:S(2)}, u32[]{:S(2)}) collective-permute-start(bf16[2,512]{1,0:T(2,128)(2,1)S(1)} %bitcast.71), channel_id=1, source_target_pairs={{0,1},{1,2},{2,3},{3,4},{4,5},{5,6},{6,7},{8,9},{9,10},{10,11},{11... | collective-permute-start | bytes 6152 | tf_op jit(solution)/shard_map/ppermute | solution.py:584
  222.3 3.3 collective-permute-start.3
  225.6 1.3 slice_bitcast_fusion.5
  226.9 0.7 slice.159
  227.6 0.7 slice.160
  228.4 0.6 pad_maximum_fusion.2.edge_ref
  229.0 7.1 %stem_back.1 = (bf16[2,512,80]{2,1,0:T(8,128)(2,1)}, f32[3,80,512]{2,1,0:T(8,128)}, f32[8,512]{1,0:T(8,128)}) custom-call(bf16[2,512,80]{2,1,0:T(8,128)(2,1)} %copy-done, bf16[2,4,80]{2,1,0:T(4,128)(2,1)} %pad_maximum_fusion.3.halo_ref, bf16[2,256,512]{2,1,0:T(8,128)(2,1)} %get-tuple-element.54.dh2_ref, bf16[2,2,512]{2,1,0:T(2,128)(2,1)} %pad_maximum_fusion.2.edge_ref, ...), custom_call_target="tpu_custom_call" | custom-call | flops 8000000000 | bytes 8000000 | tf_op jit(solution)/shard_map/stem_back/pallas_call | solution.py:534
  236.1 1.1 convert.20
  237.2 0.7 slice.161
  237.9 2.0 concatenate.28
  239.9 15.7 %all_sum4.1 = f32[8,32,512]{2,1,0:T(8,128)} custom-call(bf16[8,32,512]{2,1,0:T(8,128)(2,1)} %bitcast.60), custom_call_target="tpu_custom_call" | custom-call | tf_op jit(solution)/shard_map/all_sum4/pallas_call | solution.py:132
  255.6 1.8 slice.134
  257.4 0.8 copy.70
  258.2 1.6 fusion
  259.9 1.0 convert_element_type.25
  260.9 0.8 slice_bitcast_fusion.1
  261.7 23.2 %reduce-scatter.11.cloned.1.call-done = bf16[1,256,512]{2,1,0:T(8,128)(2,1)} async-done(((bf16[8,256,512]{2,1,0:T(8,128)(2,1)}), bf16[1,256,512]{2,1,0:T(8,128)(2,1)}) %reduce-scatter.11.cloned.1.call-update) | async-done | bytes 262160 | tf_op jit(solution)/shard_map/reduce_scatter | solution.py:579
  284.9 1.8 bitcast_convert_fusion
  286.7 30.9 %reduce-scatter.9.cloned.1.call-done = bf16[1,528,256]{2,1,0:T(8,128)(2,1)} async-done(((bf16[8,528,256]{2,1,0:T(8,128)(2,1)}), bf16[1,528,256]{2,1,0:T(8,128)(2,1)}) %reduce-scatter.9.cloned.1.call-update) | async-done | bytes 270352 | tf_op jit(solution)/shard_map/reduce_scatter | solution.py:578
  317.6 1.0 convert_element_type.26
  318.5 1.2 slice.147
  319.8 0.8 slice_bitcast_fusion
  320.6 22.0 %all-gather.8.cloned.1.call-done = bf16[8,192,512]{2,1,0:T(8,128)(2,1)} async-done(((bf16[1,192,512]{2,1,0:T(8,128)(2,1)}), bf16[8,192,512]{2,1,0:T(8,128)(2,1)}) %all-gather.8.cloned.1.call-update) | async-done | bytes 1572880 | tf_op jit(solution)/shard_map/all_gather | solution.py:587
  342.6 3.5 convert.24
  (61 shorter events, 2.9 us)
Async XLA Ops:
  7.2 7.0 %copy-start.2 = (bf16[2,512,80]{1,2,0:T(8,128)(2,1)S(1)}, bf16[2,512,80]{1,2,0:T(8,128)(2,1)}, u32[]{:S(2)}) copy-start(bf16[2,512,80]{1,2,0:T(8,128)(2,1)} %param.22) | copy-start | bytes 491524
  7.2 13.8 %copy-start.3 = (bf16[512]{0:T(512)(128)(2,1)S(1)}, bf16[512]{0:T(512)(128)(2,1)}, u32[]{:S(2)}) copy-start(bf16[512]{0:T(512)(128)(2,1)} %param.25) | copy-start | bytes 3076
  7.2 13.8 %copy-start.4 = (bf16[512]{0:T(512)(128)(2,1)S(1)}, bf16[512]{0:T(512)(128)(2,1)}, u32[]{:S(2)}) copy-start(bf16[512]{0:T(512)(128)(2,1)} %param.27) | copy-start | bytes 3076
  7.2 13.8 %copy-start.5 = (bf16[512]{0:T(512)(128)(2,1)S(1)}, bf16[512]{0:T(512)(128)(2,1)}, u32[]{:S(2)}) copy-start(bf16[512]{0:T(512)(128)(2,1)} %param.28) | copy-start | bytes 3076
  7.2 13.8 %copy-start.6 = (bf16[512]{0:T(512)(128)(2,1)S(1)}, bf16[512]{0:T(512)(128)(2,1)}, u32[]{:S(2)}) copy-start(bf16[512]{0:T(512)(128)(2,1)} %param.29) | copy-start | bytes 3076
  7.3 13.8 %copy-start.7 = (bf16[512]{0:T(512)(128)(2,1)S(1)}, bf16[512]{0:T(512)(128)(2,1)}, u32[]{:S(2)}) copy-start(bf16[512]{0:T(512)(128)(2,1)} %param.36) | copy-start | bytes 3076
  7.3 13.8 %copy-start.8 = (bf16[512]{0:T(512)(128)(2,1)S(1)}, bf16[512]{0:T(512)(128)(2,1)}, u32[]{:S(2)}) copy-start(bf16[512]{0:T(512)(128)(2,1)} %param.37) | copy-start | bytes 3076
  7.3 13.8 %copy-start.9 = (bf16[512]{0:T(512)(128)(2,1)S(1)}, bf16[512]{0:T(512)(128)(2,1)}, u32[]{:S(2)}) copy-start(bf16[512]{0:T(512)(128)(2,1)} %param.38) | copy-start | bytes 3076
  7.3 13.9 %copy-start.10 = (bf16[512]{0:T(512)(128)(2,1)S(1)}, bf16[512]{0:T(512)(128)(2,1)}, u32[]{:S(2)}) copy-start(bf16[512]{0:T(512)(128)(2,1)} %param.42) | copy-start | bytes 3076
  7.3 31.2 %all-gather.10.cloned.1.call-start = ((), (), s32[]{:S(2)}) async-start(), calls=%async_computation.9 | async-start | bytes 2949120 | tf_op jit(solution)/shard_map/all_gather | solution.py:568
  10.9 93.4 %all-gather.14.cloned.1.call-start = ((), (), s32[]{:S(2)}) async-start(), calls=%async_computation.11 | async-start | bytes 2359296 | tf_op jit(solution)/shard_map/all_gather | solution.py:570
  11.7 92.6 %all-gather.12.cloned.1.call-start = ((), (), s32[]{:S(2)}) async-start(), calls=%async_computation.10 | async-start | bytes 2433024 | tf_op jit(solution)/shard_map/all_gather | solution.py:569
  14.1 203.8 %reduce-scatter.5.cloned.1.call-start = ((), (), s32[]{:S(2)}) async-start(), calls=%async_computation.4 | async-start | bytes 1769472 | tf_op jit(solution)/shard_map/reduce_scatter | solution.py:586
  14.4 10.2 %copy-start = (bf16[2,512,80]{2,1,0:T(8,128)(2,1)}, bf16[2,512,80]{2,1,0:T(8,128)(2,1)S(1)}, u32[]{:S(2)}) copy-start(bf16[2,512,80]{2,1,0:T(8,128)(2,1)S(1)} %copy.66.mel_ref) | copy-start | bytes 491524
  14.4 7.4 %collective-permute-start = (bf16[2,2,80]{2,1,0:T(2,128)(2,1)S(1)}, bf16[2,2,80]{2,1,0:T(2,128)(2,1)S(1)}, u32[]{:S(2)}, u32[]{:S(2)}) collective-permute-start(bf16[2,2,80]{2,1,0:T(2,128)(2,1)S(1)} %get-tuple-element.163), channel_id=1, source_target_pairs={{0,1},{1,2},{2,3},{3,4},{4,5},{5,6},{6,7},{8,9},{9,10},{10,11},{11... | collective-permute-start | bytes 1928 | tf_op jit(solution)/shard_map/ppermute | solution.py:560
  19.0 4.9 %collective-permute-start.1 = (bf16[2,2,80]{2,1,0:T(2,128)(2,1)S(1)}, bf16[2,2,80]{2,1,0:T(2,128)(2,1)S(1)}, u32[]{:S(2)}, u32[]{:S(2)}) collective-permute-start(bf16[2,2,80]{2,1,0:T(2,128)(2,1)S(1)} %get-tuple-element.164), channel_id=1, source_target_pairs={{1,0},{2,1},{3,2},{4,3},{5,4},{6,5},{7,6},{9,8},{10,9},{11,10},{12... | collective-permute-start | bytes 1928 | tf_op jit(solution)/shard_map/ppermute | solution.py:561
  191.1 68.8 %reduce-scatter.7.cloned.1.call-start = ((), (), s32[]{:S(2)}) async-start(), calls=%async_computation.6 | async-start | bytes 2359296 | tf_op jit(solution)/shard_map/reduce_scatter | solution.py:585
  191.7 93.1 %reduce-scatter.11.cloned.1.call-start = ((), (), s32[]{:S(2)}) async-start(), calls=%async_computation.8 | async-start | bytes 2359296 | tf_op jit(solution)/shard_map/reduce_scatter | solution.py:579
  192.4 125.2 %reduce-scatter.9.cloned.1.call-start = ((), (), s32[]{:S(2)}) async-start(), calls=%async_computation.7 | async-start | bytes 2433024 | tf_op jit(solution)/shard_map/reduce_scatter | solution.py:578
  193.2 149.4 %all-gather.8.cloned.1.call-start = ((), (), s32[]{:S(2)}) async-start(), calls=%async_computation.5 | async-start | bytes 1769472 | tf_op jit(solution)/shard_map/all_gather | solution.py:587
  218.7 9.6 %collective-permute-start.2 = (bf16[2,512]{1,0:T(2,128)(2,1)S(1)}, bf16[2,512]{1,0:T(2,128)(2,1)S(1)}, u32[]{:S(2)}, u32[]{:S(2)}) collective-permute-start(bf16[2,512]{1,0:T(2,128)(2,1)S(1)} %bitcast.71), channel_id=1, source_target_pairs={{0,1},{1,2},{2,3},{3,4},{4,5},{5,6},{6,7},{8,9},{9,10},{10,11},{11... | collective-permute-start | bytes 6152 | tf_op jit(solution)/shard_map/ppermute | solution.py:584
  222.3 6.1 %collective-permute-start.3 = (bf16[2,512]{1,0:T(2,128)(2,1)S(1)}, bf16[2,512]{1,0:T(2,128)(2,1)S(1)}, u32[]{:S(2)}, u32[]{:S(2)}) collective-permute-start(bf16[2,512]{1,0:T(2,128)(2,1)S(1)} %bitcast.73), channel_id=1, source_target_pairs={{1,0},{2,1},{3,2},{4,3},{5,4},{6,5},{7,6},{9,8},{10,9},{11,10},{12... | collective-permute-start | bytes 6152 | tf_op jit(solution)/shard_map/ppermute | solution.py:584
  236.1 21.3 %copy-start.1 = (bf16[2,512,80]{2,1,0:T(8,128)(2,1)S(1)}, bf16[2,512,80]{2,1,0:T(8,128)(2,1)}, u32[]{:S(2)}) copy-start(bf16[2,512,80]{2,1,0:T(8,128)(2,1)} %get-tuple-element.129) | copy-start | bytes 491524
Sparse Core Ops, SparseCore 0:
  11.0 27.4 all-gather.9
  40.1 36.6 all-gather.13
  79.0 24.2 all-gather.11
  191.2 26.6 reduce-scatter.4
  220.1 31.7 reduce-scatter.6
  254.0 30.7 reduce-scatter.10
  287.8 29.7 reduce-scatter.8
  319.1 23.3 all-gather.7

commit v2 on v0

v2 whole, which is shorter than its diff:
```python
import functools
import math
import jax
import jax.numpy as jnp
from jax import lax
from jax.experimental import pallas as pl
from jax.experimental.pallas import tpu as pltpu
from jax.sharding import PartitionSpec as P

HEAD_DIM = 64
LN_EPS = 1e-5
BF = jnp.bfloat16
F32 = jnp.float32
LANES = 128
BIAS_ROWS = 16
VEC_ROWS = 8


def dims(lhs, rhs, contract_lhs, contract_rhs):
    return lax.dot_general(lhs, rhs, (((contract_lhs,), (contract_rhs,)), ((), ())), preferred_element_type=F32)


def mm(lhs, rhs):
    return dims(lhs, rhs, 1, 0)


def mm_nt(lhs, rhs):
    return dims(lhs, rhs, 1, 1)


def mm_tn(lhs, rhs):
    return dims(lhs, rhs, 0, 0)


def phi_cdf(x):
    return 0.5 * (1.0 + lax.erf(x * (0.5 ** 0.5)))


def gelu(x):
    return x * phi_cdf(x)


def gelu_grad(x):
    return phi_cdf(x) + x * (jnp.exp(x * x * -0.5) * (1.0 / math.sqrt(2.0 * math.pi)))


def norm_stats(x):
    centred = x - jnp.mean(x, axis=-1, keepdims=True)
    rstd = lax.rsqrt(jnp.mean(centred * centred, axis=-1, keepdims=True) + LN_EPS)
    return centred * rstd, rstd


def norm_back(d_out, x_hat, rstd, gain):
    a = d_out * gain
    return rstd * (a - jnp.mean(a, axis=-1, keepdims=True) - x_hat * jnp.mean(a * x_hat, axis=-1, keepdims=True))


def colsum(x):
    return jnp.sum(x, axis=0, keepdims=True)


def peer(index):
    return {'tp': index}


def entry_barrier(size, me):
    barrier = pltpu.get_barrier_semaphore()
    for step in range(1, size):
        pl.semaphore_signal(barrier, inc=1, device_id=peer(lax.rem(me + step, size)), device_id_type=pl.DeviceIdType.MESH)
    pl.semaphore_wait(barrier, size - 1)


def sibling(me):
    return me + 1 - 2 * lax.rem(me, 2)


def remote(src, dst, send_sem, recv_sem, to):
    return pltpu.make_async_remote_copy(src_ref=src, dst_ref=dst, send_sem=send_sem, recv_sem=recv_sem, device_id=peer(to),
                                        device_id_type=pl.DeviceIdType.MESH)


class Gather:
    def __init__(self, me, size, src, dst, send_sem, recv_sem):
        half = size // 2
        sib = sibling(me)
        self.first = [remote(src, dst.at[me], send_sem.at[0], recv_sem.at[0], sib)]
        self.relay = []
        for k in range(1, half):
            self.first.append(remote(src, dst.at[me], send_sem.at[k], recv_sem.at[k], lax.rem(me + 2 * k, size)))
            origin = lax.rem(me + size - 2 * k, size)
            self.relay.append(remote(dst.at[origin], dst.at[origin], send_sem.at[half + k], recv_sem.at[half + k], sib))

    def start(self):
        for copy in self.first[1:] + self.first[:1]:
            copy.start()

    def forward(self):
        for copy, onward in zip(self.first[1:], self.relay):
            copy.wait_recv()
            onward.start()

    def finish(self):
        self.first[0].wait()
        for copy in self.first[1:]:
            copy.wait_send()
        for onward in self.relay:
            onward.wait()


class Scatter:
    def __init__(self, me, size, x, own, near, far, sems, local_sem=None, part=None):
        self.half = size // 2
        self.own, self.near, self.far, self.x, self.me, self.size = own, near, far, x, me, size
        sib = sibling(me)
        send_a, recv_a, send_b, recv_b = sems
        self.stage_a = [remote(x.at[lax.rem(sib + 2 * k, size)], near.at[k], send_a.at[k], recv_a.at[k], sib)
                        for k in range(self.half)]
        self.loads = None if local_sem is None else [
            pltpu.make_async_copy(x.at[lax.rem(me + 2 * k, size)], own.at[k], local_sem.at[k]) for k in range(self.half)]
        parts = part or [(0, own.shape[1])]
        self.stage_b = [[remote(own.at[k, lo:hi], far.at[k, lo:hi], send_b.at[i, k], recv_b.at[i, k], lax.rem(me + 2 * k, size))
                         for k in range(1, self.half)] for i, (lo, hi) in enumerate(parts)]
        self.parts = parts

    def start(self):
        for copy in self.stage_a:
            copy.start()
        for load in self.loads or []:
            load.start()

    def middle(self):
        for k in range(self.half):
            if self.loads is None:
                self.own[k] = self.x[lax.rem(self.me + 2 * k, self.size)]
            else:
                self.loads[k].wait()
            self.stage_a[k].wait()
        for k in range(1, self.half):
            self.own[k] = (self.own[k].astype(F32) + self.near[k].astype(F32)).astype(BF)
        for copies in self.stage_b:
            for copy in copies:
                copy.start()

    def finish(self, i=0):
        lo, hi = self.parts[i]
        for copy in self.stage_b[i]:
            copy.wait()
        total = self.own[0, lo:hi].astype(F32) + self.near[0, lo:hi].astype(F32)
        for k in range(1, self.half):
            total = total + self.far[k, lo:hi].astype(F32)
        return total


def scatter_scratch(size, shape, parts=1):
    half = size // 2
    return [pltpu.VMEM((half,) + shape, BF)] * 3 + [pltpu.SemaphoreType.DMA((half,))] * 2 + [pltpu.SemaphoreType.DMA((parts, half))] * 2


VM = pl.BlockSpec(memory_space=pltpu.VMEM)
ANY = pl.BlockSpec(memory_space=pl.ANY)


def load_mel(m_scr, mel, halo, b):
    mel_len, n_mel = mel.shape
    total = m_scr.shape[0]
    m_scr[0:8, :] = jnp.zeros((8, m_scr.shape[1]), F32)
    m_scr[8 + mel_len:total, :] = jnp.zeros((total - 8 - mel_len, m_scr.shape[1]), F32)
    m_scr[8:8 + mel_len, 0:n_mel] = mel.astype(F32)
    m_scr[6:8, :] = halo[0, 2 * b:2 * b + 2, :]
    m_scr[8 + mel_len:10 + mel_len, :] = halo[1, 2 * b:2 * b + 2, :]


def mel_taps(m_scr, rows, n_mel):
    return [m_scr[pl.ds(5 + tap, rows, stride=2), :].astype(BF)[:, 0:n_mel] for tap in range(4)]


def conv_one(taps, w_ref, bias):
    even = mm(taps[0], w_ref[0]) + mm(taps[1], w_ref[1]) + mm(taps[2], w_ref[2]) + bias
    odd = mm(taps[1], w_ref[0]) + mm(taps[2], w_ref[1]) + mm(taps[3], w_ref[2]) + bias
    return even, odd


def row_ids(rows, width):
    return lax.broadcasted_iota(jnp.int32, (rows, width), 0)


def ring_edges(me, size, edge_ref, edge_scr, sems):
    right = remote(edge_ref.at[0], edge_scr.at[0], sems.at[0], sems.at[2], lax.rem(me + 1, size))
    left = remote(edge_ref.at[1], edge_scr.at[1], sems.at[1], sems.at[3], lax.rem(me + size - 1, size))
    return right, left


def masked_edges(me, size, edge_scr):
    side = lax.broadcasted_iota(jnp.int32, edge_scr.shape, 0)
    outside = ((side == 0) & (me == 0)) | ((side == 1) & (me == size - 1))
    return jnp.where(outside, 0.0, edge_scr[...])


def stem_kernel(size, mel_ref, edge_ref, pos_ref, w1_ref, w2_ref, vec_ref, heads_ref, h1_ref, h2_ref, x_ref, n1_ref, qkv_ref, g_ref,
                halo_ref, m_scr, e_scr, o_scr, edge_scr, edge_sem, send_sem, recv_sem):
    me = lax.axis_index('tp')
    n_batch, _, n_mel = mel_ref.shape
    frames, width = pos_ref.shape
    rows = e_scr.shape[0]
    rows3 = qkv_ref.shape[2]
    entry_barrier(size, me)
    edges = ring_edges(me, size, edge_ref, edge_scr, edge_sem)
    for copy in edges:
        copy.start()
    gather = Gather(me, size, heads_ref, g_ref, send_sem, recv_sem)
    gather.start()
    g_ref[me] = heads_ref[...]
    for copy in edges:
        copy.wait()
    halo_ref[...] = masked_edges(me, size, edge_scr)
    for b in range(n_batch):
        load_mel(m_scr, mel_ref[b], halo_ref, b)
        even, odd = conv_one(mel_taps(m_scr, rows, n_mel), w1_ref, vec_ref[0:1, :])
        e_scr[...] = gelu(even)
        o_scr[...] = gelu(odd)

        @pl.when(me == 0)
        def _():
            o_scr[0:1, :] = jnp.zeros((1, width), F32)

        h1_ref[b, :, 0:width] = o_scr[0:frames, :].astype(BF)
        h1_ref[b, :, width:2 * width] = e_scr[1:frames + 1, :].astype(BF)
        h1_ref[b, :, 2 * width:3 * width] = o_scr[1:frames + 1, :].astype(BF)
        h2_pre = mm(h1_ref[b], w2_ref[...]) + vec_ref[1:2, :]
        h2_ref[b] = h2_pre
        x_low = (gelu(h2_pre) + pos_ref[...]).astype(BF)
        x_ref[b] = x_low
        x_hat, _ = norm_stats(x_low.astype(F32))
        n1_ref[b] = (x_hat * vec_ref[2:3, :] + vec_ref[3:4, :]).astype(BF)
    gather.forward()
    gather.finish()
    w_all = g_ref[:, 0:rows3, :].reshape(size * rows3, width)
    ones = jnp.ones((BIAS_ROWS, frames), BF)
    bias = jnp.concatenate([mm_tn(g_ref[h, rows3:rows3 + BIAS_ROWS, 0:rows3], ones) for h in range(size)], axis=0)
    for b in range(n_batch):
        qkv_ref[:, b] = (mm_nt(w_all, n1_ref[b]) + bias).astype(BF).reshape(size, rows3, frames)


def stem(size, mel, edges, pos, w1, w2, vec, heads):
    n_batch, mel_len, n_mel = mel.shape
    frames, width = pos.shape
    rows = frames + 8
    rows3 = heads.shape[0] - BIAS_ROWS
    sds = jax.ShapeDtypeStruct
    return pl.pallas_call(
        functools.partial(stem_kernel, size),
        in_specs=[VM] * 7, out_specs=[VM] * 7,
        out_shape=[sds((n_batch, frames, 3 * width), BF), sds((n_batch, frames, width), F32), sds((n_batch, frames, width), BF),
                   sds((n_batch, frames, width), BF), sds((size, n_batch, rows3, frames), BF), sds((size,) + heads.shape, BF),
                   sds(edges.shape, F32)],
        scratch_shapes=[pltpu.VMEM((2 * rows + 8, LANES), F32), pltpu.VMEM((rows, width), F32), pltpu.VMEM((rows, width), F32),
                        pltpu.VMEM(edges.shape, F32), pltpu.SemaphoreType.DMA((4,)), pltpu.SemaphoreType.DMA((size,)),
                        pltpu.SemaphoreType.DMA((size,))],
        compiler_params=pltpu.CompilerParams(collective_id=0, has_side_effects=True),
        name='stem',
    )(mel, edges, pos, w1, w2, vec, heads)


def attend_kernel(size, qkv_in, w1_ref, w2_ref, o_all, o_own, p_hbm, qkv_ref, w1_all, w2_all, k_scr, v_scr, s_scr0, s_scr1, p_buf,
                  q_send, q_recv, o_send, o_recv, p_sem, w1_send, w1_recv, w2_send, w2_recv, own_sem):
    me = lax.axis_index('tp')
    parts, n_batch, rows3, frames = qkv_ref.shape
    hd = HEAD_DIM
    pairs = parts // 2
    factor = HEAD_DIM ** -0.5 * math.log2(math.e)
    scrs = (s_scr0, s_scr1)
    entry_barrier(size, me)
    arrivals = []
    for b in range(n_batch):
        arrivals.append([remote(qkv_in.at[lax.rem(me + k, size), b], qkv_ref.at[me, b], q_send.at[b, k], q_recv.at[b, k],
                                lax.rem(me + k, size)) for k in range(1, size)])
        for copy in arrivals[b]:
            copy.start()
        qkv_ref[me, b] = qkv_in[me, b]
    gathers = [Gather(me, size, w1_ref, w1_all, w1_send, w1_recv), Gather(me, size, w2_ref, w2_all, w2_send, w2_recv)]
    own = [pltpu.make_async_copy(w1_ref, w1_all.at[me], own_sem.at[0]), pltpu.make_async_copy(w2_ref, w2_all.at[me], own_sem.at[1])]
    for copy in own:
        copy.start()

    def p_copy(b, i):
        return pltpu.make_async_copy(p_buf.at[lax.rem(i, 2)], p_hbm.at[b, :, pl.ds(pl.multiple_of(i * 2 * frames, 2 * frames), 2 * frames)],
                                     p_sem.at[lax.rem(i, 2)])

    def send_out(b, i):
        for sub in range(2):
            to = 2 * i + sub

            @pl.when(to != me)
            def _():
                remote(o_own.at[to, b], o_all.at[me, b], o_send.at[b, to], o_recv.at[b, me], to).start()

            @pl.when(to == me)
            def _():
                o_all[me, b] = o_own[me, b]

    for b in range(n_batch):
        for copy in arrivals[b]:
            copy.wait()
        for part in range(parts):
            k_scr[part * frames:(part + 1) * frames, :] = qkv_ref[part, b, hd:2 * hd, :].astype(F32).T.astype(BF)
            v_scr[:, part * frames:(part + 1) * frames] = qkv_ref[part, b, 2 * hd:3 * hd, :]

        def body(i, carry):
            @pl.when(i >= 1)
            def _():
                send_out(b, i - 1)

            if b == 0:
                @pl.when(i == 1)
                def _():
                    gathers[0].start()
                    gathers[1].start()

                @pl.when(i >= 2)
                def _():
                    p_copy(b, i).wait()
            else:
                p_copy(b, i).wait()
            tops = []
            for sub in range(2):
                q_t = qkv_ref[2 * i + sub, b, 0:hd, :]
                top = None
                for part in range(parts):
                    rows = slice(part * frames, (part + 1) * frames)
                    s = mm(k_scr[rows, :], q_t)
                    scrs[sub][rows, :] = s
                    part_top = jnp.max(s.reshape(frames // 8, 8, frames), axis=0)
                    top = part_top if top is None else jnp.maximum(top, part_top)
                tops.append(jnp.max(top, axis=0, keepdims=True))
            invs = []
            for sub in range(2):
                total = jnp.zeros((8, frames), F32)
                for part in range(parts):
                    rows = slice(part * frames, (part + 1) * frames)
                    e = jnp.exp2((scrs[sub][rows, :] - tops[sub]) * factor)
                    scrs[sub][rows, :] = e
                    total = total + jnp.sum(e.reshape(frames // 8, 8, frames), axis=0)
                invs.append(1.0 / jnp.sum(total, axis=0, keepdims=True))
            for sub in range(2):
                out = jnp.zeros((hd, frames), F32)
                for part in range(parts):
                    rows = slice(part * frames, (part + 1) * frames)
                    p = (scrs[sub][rows, :] * invs[sub]).astype(BF)
                    p_buf[lax.rem(i, 2), rows, sub * frames:(sub + 1) * frames] = p
                    out = out + mm(v_scr[:, rows], p)
                o_own[2 * i + sub, b] = out.astype(BF)
            p_copy(b, i).start()
            return carry

        lax.fori_loop(0, pairs, body, 0)
        if b == n_batch - 1:
            for i in (pairs - 2, pairs - 1):
                p_copy(b, i).wait()
        send_out(b, pairs - 1)
    for gather in gathers:
        gather.forward()
    for b in range(n_batch):
        for k in range(1, size):
            to = lax.rem(me + k, size)
            remote(o_own.at[to, b], o_all.at[to, b], o_send.at[b, to], o_recv.at[b, to], to).wait()
    for gather in gathers:
        gather.finish()
    for copy in own:
        copy.wait()


def attend(size, qkv, w1, w2):
    parts, n_batch, rows3, frames = qkv.shape
    total = parts * frames
    sds = jax.ShapeDtypeStruct
    dma = pltpu.SemaphoreType.DMA
    return pl.pallas_call(
        functools.partial(attend_kernel, size),
        in_specs=[VM] * 3, out_specs=[VM, VM, ANY, VM, ANY, ANY],
        out_shape=[sds((parts, n_batch, HEAD_DIM, frames), BF), sds((parts, n_batch, HEAD_DIM, frames), BF),
                   sds((n_batch, total, total), BF), sds(qkv.shape, BF), sds((size,) + w1.shape, BF), sds((size,) + w2.shape, BF)],
        scratch_shapes=[pltpu.VMEM((total, HEAD_DIM), BF), pltpu.VMEM((HEAD_DIM, total), BF),
                        pltpu.VMEM((total, frames), F32), pltpu.VMEM((total, frames), F32), pltpu.VMEM((2, total, 2 * frames), BF),
                        dma((n_batch, size)), dma((n_batch, size)), dma((n_batch, size)), dma((n_batch, size)), dma((2,)),
                        dma((size,)), dma((size,)), dma((size,)), dma((size,)), dma((2,))],
        compiler_params=pltpu.CompilerParams(collective_id=1, has_side_effects=True),
        name='attend',
    )(qkv, w1, w2)


def attend_back_kernel(size, qkv_ref, da_ref, o_ref, p_hbm, dw1_hbm, dw2_hbm, out_all, dbias_ref, fc1_ref, fc2_ref,
                       do_scr, snd, dot_scr, do_all, q_all, delta_scr, ds_scr, p_buf, dq_scr, dv_sum,
                       a_send, a_recv, kv_send, kv_recv, dq_send, dq_recv, p_sem, load_sem,
                       own1, near1, far1, sa1, ra1, sb1, rb1, own2, near2, far2, sa2, ra2, sb2, rb2):
    me = lax.axis_index('tp')
    parts, n_batch, rows3, frames = qkv_ref.shape
    hd = HEAD_DIM
    scale = HEAD_DIM ** -0.5
    total = parts * frames
    entry_barrier(size, me)
    arrivals = []
    for b in range(n_batch):
        arrivals.append([remote(da_ref.at[lax.rem(me + k, size), b], do_scr.at[me, b], a_send.at[b, k], a_recv.at[b, k],
                                lax.rem(me + k, size)) for k in range(1, size)])
        for copy in arrivals[b]:
            copy.start()
        do_scr[me, b] = da_ref[me, b]
    scat1 = Scatter(me, size, dw1_hbm, own1, near1, far1, (sa1, ra1, sb1, rb1), load_sem.at[0])
    scat2 = Scatter(me, size, dw2_hbm, own2, near2, far2, (sa2, ra2, sb2, rb2), load_sem.at[1])
    scat1.start()
    scat2.start()

    def p_copy(b, i):
        return pltpu.make_async_copy(p_hbm.at[b, pl.ds(pl.multiple_of(i * frames, frames), frames), :], p_buf.at[lax.rem(i, 2)],
                                     p_sem.at[lax.rem(i, 2)])

    def send_piece(to, b, lo, hi, send_sem, recv_sem):
        @pl.when(to != me)
        def _():
            remote(snd.at[to, b, lo:hi], out_all.at[me, b, lo:hi], send_sem.at[b, to], recv_sem.at[b, me], to).start()

        @pl.when(to == me)
        def _():
            out_all[me, b, lo:hi, :] = snd[me, b, lo:hi, :]

    dbias_ref[...] = jnp.zeros_like(dbias_ref)
    dv_sum[...] = jnp.zeros_like(dv_sum)
    dq_rows = jnp.zeros((hd, frames), F32)
    for b in range(n_batch):
        p_copy(b, 0).start()
        for copy in arrivals[b]:
            copy.wait()
        if b == 0:
            scat1.middle()
        else:
            scat2.middle()
        for part in range(parts):
            rows = slice(part * frames, (part + 1) * frames)
            do_t = do_scr[part, b]
            dot_scr[:, rows] = do_t
            do_all[rows, :] = do_t.astype(F32).T.astype(BF)
            q_all[rows, :] = qkv_ref[part, b, 0:hd, :].astype(F32).T.astype(BF)
            delta_scr[0:1, rows] = colsum(do_t.astype(F32) * o_ref[part, b].astype(F32))
        dq_scr[...] = jnp.zeros_like(dq_scr)

        def body(i, carry):
            slot = lax.rem(i, 2)
            p_copy(b, i).wait()

            @pl.when(i + 1 < parts)
            def _():
                p_copy(b, i + 1).start()

            @pl.when(i >= 1)
            def _():
                send_piece(i - 1, b, hd, 3 * hd, kv_send, kv_recv)

            v = qkv_ref[i, b, 2 * hd:3 * hd, :].astype(F32).T.astype(BF)
            k_t = qkv_ref[i, b, hd:2 * hd, :]
            for c in range(parts // 2):
                cols = slice(c * 2 * frames, (c + 1) * 2 * frames)
                dp = mm(v, dot_scr[:, cols])
                ds = (p_buf[slot, :, cols].astype(F32) * (dp - delta_scr[0:1, cols])).astype(BF)
                ds_scr[:, cols] = ds
                dq_scr[:, cols] += mm(k_t, ds)
            dv = mm(p_buf[slot], do_all[...])
            dk = mm(ds_scr[...], q_all[...]) * scale
            dv_sum[...] += dv
            snd[i, b, hd:2 * hd, :] = dk.T.astype(BF)
            snd[i, b, 2 * hd:3 * hd, :] = dv.T.astype(BF)
            return carry

        lax.fori_loop(0, parts, body, 0)
        for part in range(parts):
            dq = dq_scr[:, part * frames:(part + 1) * frames] * scale
            dq_rows = dq_rows + dq
            snd[part, b, 0:hd, :] = dq.astype(BF)
        send_piece(parts - 1, b, hd, 3 * hd, kv_send, kv_recv)
        for part in range(parts):
            send_piece(part, b, 0, hd, dq_send, dq_recv)
    dbias_ref[0:1, :] = colsum(dq_rows.T)
    dbias_ref[1:2, :] = colsum(dv_sum[...])
    fc1_ref[...] = scat1.finish()
    fc2_ref[...] = scat2.finish()
    for b in range(n_batch):
        for k in range(1, size):
            to = lax.rem(me + k, size)
            remote(snd.at[to, b, hd:3 * hd], out_all.at[to, b, hd:3 * hd], kv_send.at[b, to], kv_recv.at[b, to], to).wait()
            remote(snd.at[to, b, 0:hd], out_all.at[to, b, 0:hd], dq_send.at[b, to], dq_recv.at[b, to], to).wait()


def attend_back(size, qkv, da, o, p, dw1, dw2):
    parts, n_batch, rows3, frames = qkv.shape
    total = parts * frames
    sds = jax.ShapeDtypeStruct
    dma = pltpu.SemaphoreType.DMA
    return pl.pallas_call(
        functools.partial(attend_back_kernel, size),
        in_specs=[VM, VM, VM, ANY, ANY, ANY], out_specs=[VM] * 4,
        out_shape=[sds(qkv.shape, BF), sds((8, HEAD_DIM), F32), sds(dw1.shape[1:], F32), sds(dw2.shape[1:], F32)],
        scratch_shapes=[pltpu.VMEM(da.shape, BF), pltpu.VMEM(qkv.shape, BF), pltpu.VMEM((HEAD_DIM, total), BF),
                        pltpu.VMEM((total, HEAD_DIM), BF), pltpu.VMEM((total, HEAD_DIM), BF), pltpu.VMEM((8, total), F32),
                        pltpu.VMEM((frames, total), BF), pltpu.VMEM((2, frames, total), BF), pltpu.VMEM((HEAD_DIM, total), F32),
                        pltpu.VMEM((frames, HEAD_DIM), F32)]
        + [dma((n_batch, size))] * 6 + [dma((2,)), dma((2, size // 2))]
        + scatter_scratch(size, dw1.shape[1:]) + scatter_scratch(size, dw2.shape[1:]),
        compiler_params=pltpu.CompilerParams(collective_id=2, has_side_effects=True),
        name='attend_back',
    )(qkv, da, o, p, dw1, dw2)


def mlp_kernel(o_ref, x_ref, dy_ref, wo_ref, w1_ref, w2_ref, vec_ref, y_ref, da_ref, dmid_ref, dwo_ref, dw1_ref, dw2_ref, dvec_ref,
               mid_scr, n2_scr, y_scr, dn_scr, hat_scr, rstd_scr):
    j = pl.program_id(0)
    heads, n_batch, hd, frames = o_ref.shape
    rows, width = x_ref.shape
    fc = dw2_ref.shape[1]
    w2 = w2_ref[0]

    @pl.when(j == 0)
    def _():
        wo = wo_ref[...].reshape(heads * hd, width)
        for b in range(n_batch):
            blk = slice(b * frames, (b + 1) * frames)
            attn = mm_tn(o_ref[:, b].reshape(heads * hd, frames), wo)
            mid = (x_ref[blk, :].astype(F32) + attn + vec_ref[4:5, :]).astype(BF)
            mid_scr[blk, :] = mid
            x_hat, rstd = norm_stats(mid.astype(F32))
            hat_scr[blk, :] = x_hat
            rstd_scr[blk, :] = jnp.broadcast_to(rstd, (frames, LANES))
            n2_scr[blk, :] = (x_hat * vec_ref[5:6, :] + vec_ref[6:7, :]).astype(BF)
        y_scr[...] = jnp.zeros_like(y_scr)
        dn_scr[...] = jnp.zeros_like(dn_scr)

    w1 = w1_ref[0, 0:width, :]
    pre = mm(n2_scr[...], w1) + w1_ref[0, width:width + 1, :].astype(F32)
    cdf = phi_cdf(pre)
    hidden = (pre * cdf).astype(BF)
    grad = cdf + pre * (jnp.exp(pre * pre * -0.5) * (1.0 / math.sqrt(2.0 * math.pi)))
    d_pre = mm_nt(dy_ref[...], w2) * grad
    d_low = d_pre.astype(BF)
    y_scr[...] += mm(hidden, w2)
    dn_scr[...] += mm_nt(d_low, w1)
    dw2_ref[0] = mm_tn(hidden, dy_ref[...]).astype(BF)
    dw1_ref[0, 0:width, :] = mm_tn(n2_scr[...], d_low).astype(BF)
    dw1_ref[0, width:width + BIAS_ROWS, :] = jnp.broadcast_to(colsum(d_pre), (BIAS_ROWS, fc)).astype(BF)

    @pl.when(j == pl.num_programs(0) - 1)
    def _():
        wo = wo_ref[...].reshape(heads * hd, width)
        y_ref[...] = (mid_scr[...].astype(F32) + y_scr[...] + vec_ref[7:8, :]).astype(BF)
        dvec_ref[...] = jnp.zeros_like(dvec_ref)
        d_wo = jnp.zeros((heads * hd, width), F32)
        for b in range(n_batch):
            blk = slice(b * frames, (b + 1) * frames)
            dy = dy_ref[blk, :].astype(F32)
            x_hat = hat_scr[blk, :]
            d_n2 = dn_scr[blk, :]
            d_mid = dy + norm_back(d_n2, x_hat, rstd_scr[blk, 0:1], vec_ref[5:6, :])
            dmid_ref[blk, :] = d_mid
            dvec_ref[0:1, :] += colsum(dy)
            dvec_ref[1:2, :] += colsum(d_n2 * x_hat)
            dvec_ref[2:3, :] += colsum(d_n2)
            dvec_ref[3:4, :] += colsum(d_mid)
            mid_low = d_mid.astype(BF)
            da_ref[:, b] = mm_nt(wo, mid_low).astype(BF).reshape(heads, hd, frames)
            d_wo = d_wo + mm(o_ref[:, b].reshape(heads * hd, frames), mid_low)
        dwo_ref[...] = d_wo.astype(BF).reshape(heads, hd, width)


def mlp(o, x, dy, w1, w2, vec):
    heads, n_batch, hd, frames = o.shape
    rows, width = x.shape
    chunks, fc = w2.shape[0], w2.shape[1] - hd
    whole = lambda shape: pl.BlockSpec(shape, lambda j: (0,) * len(shape))
    chunk = lambda shape: pl.BlockSpec((1,) + shape[1:], lambda j: (j,) + (0,) * (len(shape) - 1))
    sds = jax.ShapeDtypeStruct
    outs = [sds((rows, width), BF), sds((heads, n_batch, hd, frames), BF), sds((rows, width), F32), sds((heads, hd, width), BF),
            sds(w1.shape, BF), sds((chunks, fc, width), BF), sds((VEC_ROWS, width), F32)]
    return pl.pallas_call(
        mlp_kernel, grid=(chunks,),
        in_specs=[whole(o.shape), whole(x.shape), whole(dy.shape),
                  pl.BlockSpec((heads, hd, width), lambda j: (0, fc // hd, 0)),
                  chunk(w1.shape), chunk((chunks, fc, width)), whole(vec.shape)],
        out_specs=[whole(s.shape) for s in outs[:4]] + [chunk(w1.shape), chunk((chunks, fc, width)), whole(outs[6].shape)],
        out_shape=outs,
        scratch_shapes=[pltpu.VMEM((rows, width), BF), pltpu.VMEM((rows, width), BF), pltpu.VMEM((rows, width), F32),
                        pltpu.VMEM((rows, width), F32), pltpu.VMEM((rows, width), F32), pltpu.VMEM((rows, LANES), F32)],
        compiler_params=pltpu.CompilerParams(dimension_semantics=('arbitrary',)),
        cost_estimate=pl.CostEstimate(flops=14_000_000_000, bytes_accessed=12_000_000, transcendentals=0),
        name='mlp',
    )(o, x, dy, w2, w1, w2, vec)


def embed_back_kernel(dqkv_ref, g_ref, n1_ref, x_ref, dmid_ref, h2_ref, h1_ref, dwo_ref, vec_ref, dh2_ref, dw_ref, edge_ref, dvec_ref):
    heads, n_batch, rows3, frames = dqkv_ref.shape
    width = n1_ref.shape[2]
    w_all = g_ref[:, 0:rows3, 0:width].reshape(heads * rows3, width)
    dvec_ref[...] = jnp.zeros_like(dvec_ref)
    edge_ref[...] = jnp.zeros_like(edge_ref)
    d_all = [dqkv_ref[:, b].reshape(heads * rows3, frames) for b in range(n_batch)]
    for b in range(n_batch):
        d_n1 = mm_tn(d_all[b], w_all)
        x_hat, rstd = norm_stats(x_ref[b].astype(F32))
        d_x = dmid_ref[b * frames:(b + 1) * frames, :] + norm_back(d_n1, x_hat, rstd, vec_ref[2:3, :])
        d_h2 = d_x * gelu_grad(h2_ref[b])
        dvec_ref[0:1, :] += colsum(d_n1 * x_hat)
        dvec_ref[1:2, :] += colsum(d_n1)
        dvec_ref[2:3, :] += colsum(d_h2)
        dh2_ref[b] = d_h2.astype(BF)
        edge_ref[0, b:b + 1, :] = d_h2[frames - 1:frames].astype(BF).astype(F32)
        edge_ref[1, b:b + 1, :] = d_h2[0:1].astype(BF).astype(F32)
    d_w = mm(d_all[0], n1_ref[0])
    d_conv = mm_tn(h1_ref[0], dh2_ref[0])
    for b in range(1, n_batch):
        d_w = d_w + mm(d_all[b], n1_ref[b])
        d_conv = d_conv + mm_tn(h1_ref[b], dh2_ref[b])
    dw_ref[:, 0:rows3, :] = d_w.astype(BF).reshape(heads, rows3, width)
    dw_ref[:, rows3:rows3 + HEAD_DIM, :] = dwo_ref[...]
    dw_ref[:, rows3 + HEAD_DIM:, :] = d_conv.astype(BF).reshape(heads, 3 * width // heads, width)


def embed_back(dqkv, g, n1, x, dmid, h2, h1, dwo, vec):
    n_batch, frames, width = n1.shape
    heads = dqkv.shape[0]
    sds = jax.ShapeDtypeStruct
    return pl.pallas_call(
        embed_back_kernel,
        in_specs=[pl.BlockSpec(memory_space=pltpu.VMEM)] * 9,
        out_specs=[pl.BlockSpec(memory_space=pltpu.VMEM)] * 4,
        out_shape=[sds((n_batch, frames, width), BF), sds((heads, dqkv.shape[2] + HEAD_DIM + 3 * width // heads, width), BF), sds((2, 8, width), F32),
                   sds((VEC_ROWS, width), F32)],
        cost_estimate=pl.CostEstimate(flops=8_000_000_000, bytes_accessed=8_000_000, transcendentals=0),
        name='embed_back',
    )(dqkv, g, n1, x, dmid, h2, h1, dwo, vec)


def tail_kernel(size, mel_ref, halo_ref, dh2_ref, edge_ref, w1_ref, w2_ref, vec_ref, grads_hbm, vmlp_ref, vemb_ref,
                dmel_ref, heads_ref, conv_ref, small_ref,
                m_scr, d_scr, e_scr, o_scr, out_scr, edge_scr, sum_scr, small_scr, mine, whole, edge_sem, load_sem, g_send, g_recv,
                own1, near1, far1, sa1, ra1, sb1, rb1, own2, near2, far2, sa2, ra2, sb2, rb2):
    me = lax.axis_index('tp')
    n_batch, _, n_mel = mel_ref.shape
    frames, width = dh2_ref.shape[1:]
    rows = e_scr.shape[0]
    head_rows = heads_ref.shape[0]
    all_rows = grads_hbm.shape[1]
    conv_rows = all_rows - head_rows
    entry_barrier(size, me)
    edges = ring_edges(me, size, edge_ref, edge_scr, edge_sem)
    for copy in edges:
        copy.start()
    scat = Scatter(me, size, grads_hbm, own1, near1, far1, (sa1, ra1, sb1, rb1), load_sem,
                   part=[(head_rows, all_rows), (0, head_rows)])
    scat.start()
    small = Scatter(me, size, small_scr, own2, near2, far2, (sa2, ra2, sb2, rb2))
    for copy in edges:
        copy.wait()
    edge_scr[...] = masked_edges(me, size, edge_scr)
    sum_scr[...] = jnp.zeros_like(sum_scr)
    ids = row_ids(rows, width)
    lowest = jnp.where(me == 0, 1, 0)
    for b in range(n_batch):
        load_mel(m_scr, mel_ref[b], halo_ref, b)
        taps = mel_taps(m_scr, rows, n_mel)
        even, odd = conv_one(taps, w1_ref, vec_ref[0:1, :])
        d_scr[0:8, :] = jnp.zeros((8, width), F32)
        d_scr[frames:frames + 16, :] = jnp.zeros((16, width), F32)
        d_scr[1:frames + 1, :] = dh2_ref[b].astype(F32)
        d_scr[0:1, :] = edge_scr[0, b:b + 1, :]
        d_scr[frames + 1:frames + 2, :] = edge_scr[1, b:b + 1, :]
        here = d_scr[0:rows, :].astype(BF)
        after = d_scr[1:rows + 1, :].astype(BF)
        own = (ids >= 1) & (ids <= frames)
        d_even = jnp.where((ids >= 1) & (ids <= frames + 1), mm_nt(here, w2_ref[width:2 * width, :]) * gelu_grad(even), 0.0)
        d_odd = mm_nt(here, w2_ref[2 * width:3 * width, :]) + mm_nt(after, w2_ref[0:width, :])
        d_odd = jnp.where((ids >= lowest) & (ids <= frames), d_odd * gelu_grad(odd), 0.0)
        e_own = jnp.where(own, d_even, 0.0)
        o_own = jnp.where(own, d_odd, 0.0)
        sum_scr[3 * n_mel + 7:3 * n_mel + 8, :] += colsum(e_own) + colsum(o_own)
        e_own, o_own = e_own.astype(BF), o_own.astype(BF)
        for t in range(3):
            sum_scr[t * n_mel:(t + 1) * n_mel, :] += mm_tn(taps[t], e_own) + mm_tn(taps[t + 1], o_own)
        e_scr[...] = d_even
        o_scr[...] = d_odd
        e_here = e_scr[1:frames + 1, :].astype(BF)
        e_after = e_scr[2:frames + 2, :].astype(BF)
        o_here = o_scr[1:frames + 1, :].astype(BF)
        o_before = o_scr[0:frames, :].astype(BF)
        out_scr[pl.ds(0, frames, stride=2), 0:n_mel] = mm_nt(e_here, w1_ref[1]) + mm_nt(o_here, w1_ref[0]) + mm_nt(o_before, w1_ref[2])
        out_scr[pl.ds(1, frames, stride=2), 0:n_mel] = mm_nt(e_here, w1_ref[2]) + mm_nt(o_here, w1_ref[1]) + mm_nt(e_after, w1_ref[0])
        dmel_ref[b] = out_scr[:, 0:n_mel].astype(BF)
        if b == 0:
            scat.middle()
    sum_scr[3 * n_mel:3 * n_mel + 4, :] = vmlp_ref[0:4, :]
    sum_scr[3 * n_mel + 4:3 * n_mel + 7, :] = vemb_ref[0:3, :]
    small_scr[...] = sum_scr[...].astype(BF).reshape(small_scr.shape)
    small.start()
    small.middle()
    mine[0:conv_rows, :] = scat.finish(0).astype(BF)
    mine[conv_rows:, :] = small.finish().astype(BF)
    gather = Gather(me, size, mine, whole, g_send, g_recv)
    gather.start()
    heads_ref[...] = scat.finish(1)
    gather.forward()
    gather.finish()
    whole[me] = mine[...]
    conv_ref[...] = whole[:, 0:conv_rows, :].astype(F32)
    small_ref[...] = whole[:, conv_rows:, :].astype(F32)


def tail(size, mel, halo, dh2, edge, w1, w2, vec, grads, vmlp, vemb):
    n_batch, mel_len, n_mel = mel.shape
    frames, width = dh2.shape[1:]
    rows = frames + 8
    head_rows = 4 * HEAD_DIM
    conv_rows = grads.shape[1] - head_rows
    small_rows = -(-(3 * n_mel + 8) // (16 * size)) * 16
    half = size // 2
    sds = jax.ShapeDtypeStruct
    dma = pltpu.SemaphoreType.DMA
    return pl.pallas_call(
        functools.partial(tail_kernel, size),
        in_specs=[VM] * 7 + [ANY, VM, VM], out_specs=[VM] * 4,
        out_shape=[sds(mel.shape, BF), sds((head_rows, width), F32), sds((size, conv_rows, width), F32), sds((size, small_rows, width), F32)],
        scratch_shapes=[pltpu.VMEM((2 * rows + 8, LANES), F32), pltpu.VMEM((frames + 16, width), F32),
                        pltpu.VMEM((rows, width), F32), pltpu.VMEM((rows, width), F32), pltpu.VMEM((mel_len, LANES), F32),
                        pltpu.VMEM(edge.shape, F32), pltpu.VMEM((size * small_rows, width), F32),
                        pltpu.VMEM((size, small_rows, width), BF), pltpu.VMEM((conv_rows + small_rows, width), BF),
                        pltpu.VMEM((size, conv_rows + small_rows, width), BF), dma((4,)), dma((half,)), dma((size,)), dma((size,))]
        + scatter_scratch(size, grads.shape[1:], 2) + scatter_scratch(size, (small_rows, width)),
        compiler_params=pltpu.CompilerParams(collective_id=3, has_side_effects=True),
        name='tail',
    )(mel, halo, dh2, edge, w1, w2, vec, grads, vmlp, vemb)


def device_step(mel_in, pos_table, w_conv1, b_conv1, w_conv2, b_conv2, ln1_gain, ln1_bias, w_query, b_query,
                w_key, w_value, b_value, w_out, b_out, ln2_gain, ln2_bias, w_fc1, b_fc1, w_fc2, b_fc2, grad_y,
                group_size):
    n_batch, mel_len, n_mel = mel_in.shape
    frames, width = pos_table.shape
    fc = w_fc1.shape[1]
    hd = w_query.shape[1]
    rows3 = 3 * hd
    rows = n_batch * frames
    edges = jnp.stack([mel_in[:, -2:], mel_in[:, :2]]).astype(F32).reshape(2, 2 * n_batch, n_mel)
    edges = jnp.pad(edges, ((0, 0), (0, 8 - 2 * n_batch), (0, LANES - n_mel)))
    vec = jnp.stack([b_conv1, b_conv2, ln1_gain, ln1_bias, b_out, ln2_gain, ln2_bias, b_fc2]).astype(F32)
    w2_flat = w_conv2.reshape(3 * width, width)
    bias = jnp.concatenate([b_query, jnp.zeros_like(b_query), b_value])
    bias = jnp.pad(bias[None], ((0, BIAS_ROWS - 1), (0, width - rows3)))
    heads_w = jnp.concatenate([jnp.concatenate([w_query, w_key, w_value], axis=1).T, bias], axis=0)
    fc1_w = jnp.concatenate([w_fc1, jnp.broadcast_to(b_fc1[None], (BIAS_ROWS, fc))], axis=0)
    fc2_w = jnp.concatenate([w_fc2, w_out], axis=0)

    h1, h2_pre, x_embed, norm_one, qkv_send, heads_all, halo = stem(group_size, mel_in, edges, pos_table, w_conv1, w2_flat, vec, heads_w)
    o_all, o_heads, probs, qkv, fc1_all, fc2_all = attend(group_size, qkv_send, fc1_w, fc2_w)
    y_out, d_attn, d_mid, d_wo, d_fc1, d_fc2, vec_mlp = mlp(
        o_all, x_embed.reshape(rows, width), grad_y.reshape(rows, width), fc1_all, fc2_all, vec)
    d_qkv, d_bias, fc1_own, fc2_own = attend_back(group_size, qkv, d_attn, o_heads, probs, d_fc1, d_fc2)
    d_h2, d_w, d_edge, vec_embed = embed_back(d_qkv, heads_all, norm_one, x_embed, d_mid, h2_pre, h1, d_wo, vec)
    d_mel, heads_own, d_conv2, small = tail(group_size, mel_in, halo, d_h2, d_edge, w_conv1, w2_flat, vec, d_w, vec_mlp, vec_embed)
    small = small.reshape(-1, width)
    d_conv1 = small[:3 * n_mel].reshape(w_conv1.shape)
    vecs = small[3 * n_mel:]
    return (y_out.reshape(grad_y.shape), d_mel, d_conv1, vecs[7], d_conv2.reshape(w_conv2.shape), vecs[6], vecs[4], vecs[5],
            heads_own[0:hd].T, d_bias[0], heads_own[hd:2 * hd].T, heads_own[2 * hd:3 * hd].T, d_bias[1],
            heads_own[3 * hd:], vecs[3], vecs[1], vecs[2], fc1_own[:width], fc1_own[width], fc2_own, vecs[0])


def solution(mesh):
    group_size = mesh.shape['tp']
    in_specs = (P('dp', 'tp', None), P('tp', None), P(), P(), P(), P(), P(), P(),
                P(None, 'tp'), P('tp'), P(None, 'tp'), P(None, 'tp'), P('tp'), P('tp', None), P(), P(), P(),
                P(None, 'tp'), P('tp'), P('tp', None), P(), P('dp', 'tp', None))
    out_specs = (P('dp', 'tp', None), P('dp', 'tp', None), P('dp', None, None), P('dp'), P('dp', None, None),
                 P('dp'), P('dp'), P('dp'), P('dp', 'tp'), P(('dp', 'tp')), P('dp', 'tp'), P('dp', 'tp'),
                 P(('dp', 'tp')), P(('dp', 'tp'), None), P('dp'), P('dp'), P('dp'), P('dp', 'tp'),
                 P(('dp', 'tp')), P(('dp', 'tp'), None), P('dp'))
    local_step = functools.partial(device_step, group_size=group_size)
    return jax.shard_map(local_step, mesh=mesh, in_specs=in_specs, out_specs=out_specs, check_vma=False)
```

time: 610 us -> 237 us (0.39); the launches traced: 601 us -> 237 us
  waiting for transfers between devices: 238 us -> 0 us
  matrix products: 215 us -> 0 us
  Pallas kernels: 0 us -> 207 us
  blocking collectives: 64.5 us -> 0 us
  other arithmetic: 40.6 us -> 6.06 us
  between operations: 15.4 us -> 0.75 us
    pallas_call x0 -> x6, Pallas kernels: none -> 207 us  [the longest x1 56.2 us: attend(): pl.pallas_call(functools.partial(attend_kernel, size), in_specs=[VM] * 3,...]
    dot_general x31 -> x0, matrix products: 200 us -> none  [contract(): return jnp.einsum(pattern, lhs, rhs, preferred_element_type=jnp.float32)]
    reduce_scatter x4 -> x0, waiting for transfers between devices: 113 us -> none  [the longest x1 32.3 us: device_step(): lax.psum_scatter(contract('btf,fd->btd', fc_hidden, w_fc2).astype(jnp.bfl...]
    all_gather x4 -> x0, waiting for transfers between devices: 105 us -> none  [the longest x1 31.1 us: device_step(): norm_one_all = lax.all_gather(norm_one, 'tp', axis=1, tiled=True)]
    all_gather x3 -> x0, blocking collectives: 44 us -> none  [the longest x1 16.3 us: device_step(): tap_edges = lax.all_gather(d_taps[:, 0, 0], 'tp')]
    psum x1 -> x0, blocking collectives: 20.5 us -> none  [device_step(): lax.psum((d_w_conv1, d_b_conv1, d_w_conv2, d_b_conv2, d_ln1_gain, d_ln1_b...]
    psum x1 -> x0, waiting for transfers between devices: 19.6 us -> none  [device_step(): lax.psum((d_w_conv1, d_b_conv1, d_w_conv2, d_b_conv2, d_ln1_gain, d_ln1_b...]
    reduce_sum x10 -> x0, other arithmetic: 18.9 us -> none  [the longest x4 8.76 us: norm_f32(): return centred * lax.rsqrt(row_var + LN_EPS) * gain_vec + shift_vec]
  transfers between devices with their start and end apart: 9 -> 0, of which waited for: 9 -> 0; matrix products, arithmetic and copies ran while one was open for 6% -> 0% of each run, Pallas kernels for 0% -> 0%
where the time goes in v2:
time: 237 us
  Pallas kernels  207 us (87%)
  local copies, waits for them, and re-layouts  23.1 us (10%)
  other arithmetic  6.06 us (3%)
    pallas_call x1, Pallas kernels, attend(): pl.pallas_call(functools.partial(attend_kernel, size), in_specs=[VM] * 3,...  56.2 us
    pallas_call x1, Pallas kernels, attend_back(): pl.pallas_call(functools.partial(attend_back_kernel, size), in_specs=[VM,...  53.9 us
    pallas_call x1, Pallas kernels, tail(): pl.pallas_call(functools.partial(tail_kernel, size), in_specs=[VM] * 7 +...  49.5 us
    pallas_call x1, Pallas kernels, stem(): pl.pallas_call(functools.partial(stem_kernel, size), in_specs=[VM] * 7, o...  22.6 us
    pallas_call x1, Pallas kernels, mlp(): pl.pallas_call(mlp_kernel, grid=(chunks,), in_specs=[whole(o.shape), whol...  15.7 us
    pallas_call x1, Pallas kernels, embed_back(): pl.pallas_call(embed_back_kernel, in_specs=[pl.BlockSpec(memory_space=plt...  8.66 us
    unnamed x12, local copies, waits for them, and re-layouts  6.12 us
    another operation x9, local copies, waits for them, and re-layouts, device_step(): jnp.stack([b_conv1, b_conv2, ln1_gain, ln1_bias, b_out, ln2_gain, ln2_bia...  5.49 us

profile of v2, /device:TPU:81, one launch (start us, length us, event | category | flops | bytes accessed | tf_op | source)
XLA Modules:
  0.0 236.5 jit_solution(16216022642470033305)
XLA Ops:
  0.7 0.0 copy-start.2
  0.7 0.0 copy-start.3
  0.7 0.8 pad_maximum_fusion.2
  1.5 0.7 stack.39
  2.2 0.7 stack.40
  2.9 0.7 stack.41
  3.5 0.7 stack.42
  4.2 0.7 stack.43
  4.9 0.7 stack.44
  5.6 0.7 stack.45
  6.3 0.7 stack.46
  7.0 0.6 convert_element_type.9.vec_ref
  7.6 0.7 broadcast_in_dim.14
  8.3 0.9 fusion.11
  9.1 0.1 copy.43
  9.2 0.1 copy.44
  9.3 0.6 fusion.8.edge_ref
  10.0 0.9 maximum_bitcast_fusion
  10.9 0.7 fusion.1.heads_ref
  11.6 1.7 copy.45.mel_ref
  13.3 1.7 pad_maximum_fusion.1.w1_ref
  15.0 0.0 copy-done.2
  15.0 0.0 copy-done.3
  15.0 0.7 pad_maximum_fusion.w2_ref
  15.7 22.6 %stem.1 = (bf16[2,256,1536]{2,1,0:T(8,128)(2,1)}, f32[2,256,512]{2,1,0:T(8,128)}, bf16[2,256,512]{2,1,0:T(8,128)(2,1)}, bf16[2,256,512]{2,1,0:T(8,128)(2,1)}, bf...) custom-call(bf16[2,512,80]{2,1,0:T(8,128)(2,1)} %copy.45.mel_ref, ...), custom_call_target="tpu_custom_call" | custom-call | tf_op jit(solution)/shard_map/stem/pallas_call | solution.py:250
  38.4 56.2 %attend.1 = (bf16[8,2,64,256]{3,2,1,0:T(8,128)(2,1)}, bf16[8,2,64,256]{3,2,1,0:T(8,128)(2,1)}, bf16[2,2048,2048]{2,1,0:T(8,128)(2,1)}, bf16[8,2,192,256]{3,2,1,0...) custom-call(bf16[8,2,192,256]{3,2,1,0:T(8,128)(2,1)} %get-tuple-element.53.qkv_in, ...), custom_call_target="tpu_custom_call" | custom-call | tf_op jit(solution)/shard_map/attend/pallas_call | solution.py:377
  94.6 15.7 %mlp.1 = (bf16[512,512]{1,0:T(8,128)(2,1)}, bf16[8,2,64,256]{3,2,1,0:T(8,128)(2,1)}, f32[512,512]{1,0:T(8,128)}, bf16[8,64,512]{2,1,0:T(8,128)(2,1)}, bf16[8,528...) custom-call(bf16[8,2,64,256]{3,2,1,0:T(8,128)(2,1)} %get-tuple-element.54.o_ref, ...), custom_call_target="tpu_custom_call" | custom-call | flops 14000000000 | bytes 12000000 | tf_op jit(solution)/shard_map/mlp/pallas_call | solution.py:580
  110.3 53.9 %attend_back.1 = (bf16[8,2,192,256]{3,2,1,0:T(8,128)(2,1)}, f32[8,64]{1,0:T(8,128)}, f32[528,256]{1,0:T(8,128)}, f32[256,512]{1,0:T(8,128)}) custom-call(bf16[8,2,192,256]{3,2,1,0:T(8,128)(2,1)} %get-tuple-element.60.qkv_ref, bf16[8,2,64,256]{3,2,1,0:T(8,128)(2,1)} %get-tuple-element.61.da_ref, bf16[8,2,64,256]{3,2,1,0:T(8,128)(2,1)} %get-tuple-element.62.o_ref, ...), custom_call_target="tpu_custom_call" | custom-call | tf_op jit(solution)/shard_map/attend_back/pallas_call | solution.py:497
  164.2 8.7 %embed_back.1 = (bf16[2,256,512]{2,1,0:T(8,128)(2,1)}, bf16[8,448,512]{2,1,0:T(8,128)(2,1)}, f32[2,8,512]{2,1,0:T(8,128)}, f32[8,512]{1,0:T(8,128)}) custom-call(bf16[8,2,192,256]{3,2,1,0:T(8,128)(2,1)} %get-tuple-element.66.dqkv_ref, bf16[8,208,512]{2,1,0:T(8,128)(2,1)} %get-tuple-element.67.g_ref, bf16[2,256,512]{2,1,0:T(8,128)(2,1)} %get-tuple-element.68.n1_ref, ...), custom_call_target="tpu_custom_call" | custom-call | flops 8000000000 | bytes 8000000 | tf_op jit(solution)/shard_map/embed_back/pallas_call | solution.py:627
  172.9 49.5 %tail.1 = (bf16[2,512,80]{2,1,0:T(8,128)(2,1)}, f32[256,512]{1,0:T(8,128)}, f32[8,192,512]{2,1,0:T(8,128)}, f32[8,32,512]{2,1,0:T(8,128)}) custom-call(bf16[2,512,80]{2,1,0:T(8,128)(2,1)} %copy.45.mel_ref, f32[2,8,128]{2,1,0:T(8,128)} %get-tuple-element.59.halo_ref, bf16[2,256,512]{2,1,0:T(8,128)(2,1)} %get-tuple-element.73.dh2_ref, ...), custom_call_target="tpu_custom_call" | custom-call | tf_op jit(solution)/shard_map/tail/pallas_call | solution.py:722
  222.4 0.0 copy-start
  222.4 1.9 copy.47
  224.3 1.3 slice.83
  225.6 1.9 slice.82
  227.5 1.3 slice_bitcast_fusion.3
  228.7 1.6 fusion.9
  230.4 1.8 slice.85
  232.2 1.9 fusion.10
  234.1 0.0 copy-done
  234.1 0.0 copy-start.1
  234.1 1.7 copy.50
  235.7 0.0 copy-done.1
  235.8 0.8 copy.51
  (3 shorter events, 0.0 us)
Async XLA Ops:
  0.7 14.3 %copy-start.2 = (bf16[256,512]{1,0:T(8,128)(2,1)S(1)}, bf16[256,512]{1,0:T(8,128)(2,1)}, u32[]{:S(2)}) copy-start(bf16[256,512]{1,0:T(8,128)(2,1)} %param.41) | copy-start | bytes 786436
  0.7 14.3 %copy-start.3 = (bf16[64,512]{1,0:T(8,128)(2,1)S(1)}, bf16[64,512]{1,0:T(8,128)(2,1)}, u32[]{:S(2)}) copy-start(bf16[64,512]{1,0:T(8,128)(2,1)} %param.35) | copy-start | bytes 196612
  222.4 11.7 %copy-start = (f32[8,192,512]{2,1,0:T(8,128)S(1)}, f32[8,192,512]{2,1,0:T(8,128)}, u32[]{:S(2)}) copy-start(f32[8,192,512]{2,1,0:T(8,128)} %get-tuple-element.80) | copy-start | bytes 9437188
  234.1 1.7 copy-start.1
